TPU v7x, 32 devices: a whole 2x2x4 slice. The times are simulated.
32 devices in a mesh: grp: 2 (over y), tile: 4 (over z), coil: 2 (over x), spk: 2 (over core).
Axes of the slice: x: 2, y: 2, z: 4, core: 2. Of those that a mesh axis runs over, the one named last changes fastest.
Arguments:
- coil_maps: float32 [2, 512, 2, 256], P('coil', ('grp', 'tile', 'spk')), parts along dimension 1, may hold values from -6 to 6
- kspace_data: bfloat16 [2, 128, 2, 256], P('coil', ('grp', 'tile', 'spk')), parts along dimension 1, may hold values from -24 to 24
- interp_weights: bfloat16 [128, 6, 256], P(('grp', 'tile', 'spk')), parts along dimension 0, may hold values from 0.099609375 to 1
- sample_bins: int32 [128, 256], P(('grp', 'tile', 'spk')), parts along dimension 0, may hold values from 0 to 65535, as said below
- spoke_count: int32 [16], P(('grp', 'tile', 'spk')), parts along dimension 0, may hold values from 1 to 8, 32 in all
- thresholds: float32 [3], replicated, may hold values from 0.05 to 0.3
Outputs:
- image: float32 [512, 2, 256], P(('grp', 'tile', 'spk')), parts along dimension 0
There are 2 independent parts, one for each index of `grp`. A program takes and returns all parts, laid end to end along the dimension named above; an argument that names none is the same for every part. Nothing has to cross between parts.
Inputs may be any that keep to these rules, and one draw needn't show every extreme that they name: `sample_bins`: sample k of each spoke lies on a straight line through cell (128, 128), at offset k - 128 along the spoke's direction, coordinates taken modulo 256. `spoke_count`: each independent slice has its own 8 counts, and the whole array holds one such block of counts per slice. The 8 counts of each slice sum to 32. In every draw, at least one device of each slice holds 8 live spokes. A device's live spokes are its first ones.
All inputs are finite; a program needn't handle non-finite values.
Results may differ from a plain program's by a relative error of at most 0.0016.
Values may be sent and summed in bfloat16 or wider, within the bound.
A program may use at most 64 MiB of HBM per device.

v0:
```python
import functools
import math

import jax
import jax.numpy as jnp
import numpy as np
from jax import lax
from jax.experimental import pallas as pl
from jax.experimental.pallas import tpu as pltpu
from jax.sharding import PartitionSpec as P

SPK_DEV = 8
LEVELS = 3
ITERS = 4
CORES = 2
CHUNKS = 2
GROUP = 4
STEP_SIZE = 0.5
LANES = 128
F32 = jnp.float32
BF16 = jnp.bfloat16
MESH = pl.DeviceIdType.MESH


def split_np(table):
    high = table.astype(jnp.bfloat16)
    low = (table - high.astype(np.float32)).astype(jnp.bfloat16)
    return high, low


def haar_signs(length, levels):
    mat = np.eye(length)
    for level in range(levels):
        span = length >> level
        half = span // 2
        step = np.eye(length)
        step[:span] = 0.0
        for i in range(half):
            step[i, 2 * i] = step[i, 2 * i + 1] = 1.0
            step[half + i, 2 * i] = 1.0
            step[half + i, 2 * i + 1] = -1.0
        mat = step @ mat
    return mat


def haar_labels(length, levels):
    label = np.ones((length,), np.int32)
    for level in range(1, levels + 1):
        label = label + (np.arange(length) < length >> level)
    return label


def tables(n, levels, chunk):
    phase = np.outer(np.arange(n), np.arange(n)) % n
    angle = phase * (2.0 * np.pi / n)
    cosine = (np.cos(angle) / math.sqrt(n)).astype(np.float32)
    sine = (np.sin(angle) / math.sqrt(n)).astype(np.float32)
    wide = np.concatenate([cosine, sine], axis=1)
    tall = np.concatenate([cosine, sine], axis=0)
    col = haar_signs(n, levels)
    block = 2**levels
    small = haar_signs(block, levels)
    rows = np.kron(np.eye(chunk // block), small)
    col_norm = 1.0 / np.sqrt((col**2).sum(1))
    row_norm = 1.0 / np.sqrt((small**2).sum(1))
    scale = np.tile(row_norm[:, None] * col_norm[None, :], (chunk // block, 1))
    label = np.minimum(haar_labels(block, levels)[:, None], haar_labels(n, levels)[None, :])
    label = np.tile(label, (chunk // block, 1))
    wide_h, wide_l = split_np(wide)
    tall_h, tall_l = split_np(tall)
    as_bf = lambda a: np.ascontiguousarray(a).astype(jnp.bfloat16)
    return (
        wide_h, wide_l, tall_h, tall_l,
        as_bf(col.T), as_bf(col), as_bf(rows), as_bf(rows.T),
        np.ascontiguousarray(scale.T).astype(np.float32), np.ascontiguousarray(label.T).astype(np.int32),
    )


def split(x):
    high = x.astype(BF16)
    return high, (x - high.astype(F32)).astype(BF16)


def mm(a, b):
    return jnp.dot(a, b, preferred_element_type=F32)


def mm3(a, b):
    return mm(a[0], b[0]) + (mm(a[0], b[1]) + mm(a[1], b[0]))


def kernel(
    dims,
    thr_ref, meta_ref, data_ref, map_ref,
    wide_h, wide_l, tall_h, tall_l, col_t, col_m, row_m, row_t, scale_ref, label_ref,
    out_ref,
    meta_all, data_all, maps, comp, comp_data, row_tab, col_tab, kspace, grid, back_h, back_l,
    half_h, half_l, estimate, grads, sens,
    meta_send, meta_recv, data_send, data_recv, map_send, map_recv, grad_send, grad_recv,
):
    n, tiles, coils, rows, live = dims
    blocks = tiles * CORES
    chunk = n // CHUNKS
    coil, tile, core = lax.axis_index("coil"), lax.axis_index("tile"), lax.axis_index("spk")
    pair, bit = coil // CORES, coil % CORES
    block = tile * CORES + core
    mine = pair * CORES + core

    barrier = pltpu.get_barrier_semaphore()
    peers = [
        (d_bit, d_tile, d_core)
        for d_bit in range(CORES)
        for d_tile in range(tiles)
        for d_core in range(CORES)
        if d_bit + d_tile + d_core > 0
    ]
    for d_bit, d_tile, d_core in peers:
        pl.semaphore_signal(
            barrier,
            inc=1,
            device_id={
                "coil": pair * CORES + (bit + d_bit) % CORES,
                "tile": (tile + d_tile) % tiles,
                "spk": (core + d_core) % CORES,
            },
            device_id_type=MESH,
        )
    for d in range(CORES, coils):
        pl.semaphore_signal(
            barrier,
            inc=1,
            device_id={
                "coil": (coil + d // CORES * CORES) % coils,
                "spk": (core + d % CORES) % CORES,
            },
            device_id_type=MESH,
        )
    pl.semaphore_wait(barrier, len(peers) + coils - CORES)

    sends = []
    for d_tile in range(tiles):
        for d_core in range(CORES):
            if d_tile == 0 and d_core == 0:
                continue
            copy = pltpu.make_async_remote_copy(
                src_ref=meta_ref,
                dst_ref=meta_all.at[block],
                send_sem=meta_send.at[d_tile * CORES + d_core],
                recv_sem=meta_recv.at[block],
                device_id={"tile": (tile + d_tile) % tiles, "spk": (core + d_core) % CORES},
                device_id_type=MESH,
            )
            copy.start()
            sends.append(copy)
    across_core = []
    for src, dst, s_sem, r_sem in (
        (data_ref, data_all.at[block], data_send, data_recv),
        (map_ref, maps.at[:, block], map_send, map_recv),
    ):
        for d_bit in range(CORES):
            for d_tile in range(tiles):
                copy = pltpu.make_async_remote_copy(
                    src_ref=src,
                    dst_ref=dst,
                    send_sem=s_sem.at[d_bit * tiles + d_tile],
                    recv_sem=r_sem.at[block],
                    device_id={
                        "coil": pair * CORES + (bit + d_bit) % CORES,
                        "tile": (tile + d_tile) % tiles,
                        "spk": bit,
                    },
                    device_id_type=MESH,
                )
                if d_bit == 0 and d_tile == 0:
                    local_copy = pltpu.make_async_copy(src, dst, r_sem.at[block])

                    @pl.when(core == bit)
                    def _(local_copy=local_copy):
                        local_copy.start()

                    @pl.when(core != bit)
                    def _(copy=copy):
                        copy.start()

                    across_core.append(copy)
                else:
                    copy.start()
                    sends.append(copy)

    meta_all[block] = meta_ref[...]
    for d_block in range(1, blocks):
        other = (block + d_block) % blocks
        pltpu.make_async_copy(meta_all.at[other], meta_all.at[other], meta_recv.at[other]).wait()

    slots = blocks * SPK_DEV * 2
    packed = meta_all[...].reshape(slots, meta_ref.shape[1])
    up = lax.broadcasted_iota(jnp.int32, (slots, slots), 0) // 2
    across = lax.broadcasted_iota(jnp.int32, (slots, slots), 1) // 2
    parity = lax.broadcasted_iota(jnp.int32, (slots, LANES), 0) % 2
    flag = jnp.where((packed[:, :LANES].astype(F32) >= 0.0) & (parity == 0), 1.0 / LANES, 0.0)
    flags = lax.dot_general(
        jnp.ones((LANES, LANES), BF16), flag.astype(BF16), (((1,), (1,)), ((), ())),
        preferred_element_type=F32,
    ).astype(BF16)
    rank = mm(flags, jnp.where(up < across, 1.0, 0.0).astype(BF16))
    alive = mm(flags, jnp.where(up == across, 1.0, 0.0).astype(BF16))
    place = lax.broadcasted_iota(jnp.int32, (LANES, slots), 0)
    which = lax.broadcasted_iota(jnp.int32, (LANES, slots), 1) % 2
    hit = (alive > 0.5) & (rank.astype(jnp.int32) == place)
    pick = [jnp.where(hit & (which == h), 1.0, 0.0).astype(BF16) for h in range(2)]
    for h in range(2):
        comp[h] = mm(pick[h], packed)

    cells = lax.broadcasted_iota(jnp.int32, (n, n), 0)

    def build(i, carry):
        def table(centre, weights):
            gap = (cells - centre.astype(jnp.int32) + 1) & (n - 1)
            return jnp.where(
                gap == 0, weights[0], jnp.where(gap == 1, weights[1], jnp.where(gap == 2, weights[2], 0.0))
            ).astype(BF16)

        def part(h, j):
            return comp[h, pl.ds(i, 1), j * n : (j + 1) * n]

        row_tab[i] = table(part(0, 0), (part(0, 2), part(0, 3), part(1, 0)))
        col_tab[i] = table(part(0, 1), (part(1, 1), part(1, 2), part(1, 3)))
        return carry

    lax.fori_loop(0, live, build, 0)

    for b in range(blocks):
        pltpu.make_async_copy(data_all.at[b], data_all.at[b], data_recv.at[b]).wait()
    samples = data_all[...].reshape(slots, n)
    for h in range(2):
        comp_data[h] = mm(pick[h], samples)

    offset = jnp.abs(lax.broadcasted_iota(jnp.int32, (1, n), 1) - n // 2).astype(F32)
    density = (offset + 0.5) * (n / (3.0 * n * live))
    wide = (wide_h[...], wide_l[...])
    tall = (tall_h[...], tall_l[...])

    for it in range(ITERS):
        slot = it % 2
        grid[...] = jnp.zeros_like(grid)

        def spokes(step, carry, it=it):
            total = None
            for g in range(GROUP):
                i = step * GROUP + g
                real = -comp_data[0, pl.ds(i, 1), :]
                imag = -comp_data[1, pl.ds(i, 1), :]
                col = col_tab[i].astype(F32)
                if it > 0:
                    inner = mm(kspace[...], row_tab[i])
                    real = real + jnp.sum(inner[:n] * col, axis=0, keepdims=True)
                    imag = imag + jnp.sum(inner[n:] * col, axis=0, keepdims=True)
                real, imag = density * real, density * imag
                smeared = jnp.concatenate(
                    [(col * real).astype(BF16), (col * imag).astype(BF16)], axis=0
                )
                added = lax.dot_general(
                    smeared, row_tab[i], (((1,), (1,)), ((), ())), preferred_element_type=F32
                )
                total = added if total is None else total + added
            grid[...] += total
            return carry

        lax.fori_loop(0, live // GROUP, spokes, 0)

        turned = mm3(split(grid[...]), wide)
        for p, value in enumerate(
            (turned[:n, :n] - turned[n:, n:], turned[:n, n:] + turned[n:, :n])
        ):
            back_h[p], back_l[p] = split(value)
        if it == 0:
            for b in range(blocks):
                pltpu.make_async_copy(maps.at[:, b], maps.at[:, b], map_recv.at[b]).wait()

            per_chunk = blocks // CHUNKS
            for p in range(2):
                for q in range(CHUNKS):
                    part = maps[p, q * per_chunk : (q + 1) * per_chunk].reshape(chunk, n)
                    sens[p, q] = part.T

        copies = []
        for q in range(CHUNKS):
            rs = slice(q * chunk, (q + 1) * chunk)
            b_h = jnp.concatenate([back_h[0, :, rs], back_h[1, :, rs]], axis=1)
            b_l = jnp.concatenate([back_l[0, :, rs], back_l[1, :, rs]], axis=1)
            image = mm3(tall, (b_h, b_l))
            d_r = image[:n, :chunk] - image[n:, chunk:]
            d_i = image[:n, chunk:] + image[n:, :chunk]
            m_r, m_i = sens[0, q], sens[1, q]
            grads[slot, q, mine, 0] = m_r * d_r + m_i * d_i
            grads[slot, q, mine, 1] = m_r * d_i - m_i * d_r
            for d in range(1, coils):
                d_pair, d_core = d // CORES, d % CORES
                copy = pltpu.make_async_remote_copy(
                    src_ref=grads.at[slot, q, mine],
                    dst_ref=grads.at[slot, q, mine],
                    send_sem=grad_send.at[slot, q, d],
                    recv_sem=grad_recv.at[slot, q, mine],
                    device_id={
                        "coil": (coil + d_pair * CORES) % coils,
                        "spk": (core + d_core) % CORES,
                    },
                    device_id_type=MESH,
                )
                copy.start()
                copies.append(copy)

        limits = jnp.ones((n, chunk), F32)
        label = label_ref[...]
        for level in range(LEVELS):
            limits = jnp.where(label == level + 1, thr_ref[level], limits)
        active = label <= LEVELS
        scale = scale_ref[...]
        for q in range(CHUNKS):
            for d in range(1, coils):
                d_pair, d_core = d // CORES, d % CORES
                other = (coil + d_pair * CORES) % coils // CORES * CORES + (core + d_core) % CORES
                pltpu.make_async_copy(
                    grads.at[slot, q, other], grads.at[slot, q, other], grad_recv.at[slot, q, other]
                ).wait()
            summed = grads[slot, q, 0]
            for c in range(1, coils):
                summed = summed + grads[slot, q, c]
            rs = slice(q * chunk, (q + 1) * chunk)
            target = -STEP_SIZE * summed
            if it > 0:
                target = estimate[:, q] + target
            side = split(jnp.concatenate([target[0], target[1]], axis=1))
            along = mm(col_m[...], side[0]) + mm(col_m[...], side[1])
            side = split(jnp.concatenate([along[:, :chunk], along[:, chunk:]], axis=0))
            coeffs = mm(side[0], row_t[...]) + mm(side[1], row_t[...])
            c_r, c_i = coeffs[:n] * scale, coeffs[n:] * scale
            size = jnp.sqrt(c_r * c_r + c_i * c_i)
            factor = jnp.maximum(size - limits, 0.0) / jnp.maximum(size, limits)
            factor = jnp.where(active, factor, 1.0) * scale
            side = split(jnp.concatenate([c_r * factor, c_i * factor], axis=0))
            along = mm(side[0], row_m[...]) + mm(side[1], row_m[...])
            side = split(jnp.concatenate([along[:n], along[n:]], axis=1))
            fresh = mm(col_t[...], side[0]) + mm(col_t[...], side[1])
            e_r, e_i = fresh[:, :chunk], fresh[:, chunk:]
            estimate[0, q] = e_r
            estimate[1, q] = e_i
            if it < ITERS - 1:
                m_r, m_i = sens[0, q], sens[1, q]
                seen = split(
                    jnp.concatenate([m_r * e_r - m_i * e_i, m_r * e_i + m_i * e_r], axis=1)
                )
                w = mm3(tall, seen)
                half = jnp.concatenate(
                    [w[:n, :chunk] + w[n:, chunk:], w[:n, chunk:] - w[n:, :chunk]], axis=0
                )
                half_h[:, rs], half_l[:, rs] = split(half)
            else:
                per_chunk = blocks // CHUNKS
                maps[0, q * per_chunk : (q + 1) * per_chunk] = e_r.T.reshape(per_chunk, rows, n)
                maps[1, q * per_chunk : (q + 1) * per_chunk] = e_i.T.reshape(per_chunk, rows, n)
        for copy in copies:
            copy.wait_send()
        if it < ITERS - 1:
            v = mm3((half_h[...], half_l[...]), wide)
            kspace[:n, :] = (v[:n, :n] + v[n:, n:]).astype(BF16)
            kspace[n:, :] = (v[n:, :n] - v[:n, n:]).astype(BF16)

    out_ref[...] = maps[:, block]

    @pl.when(core != bit)
    def _():
        for copy in across_core:
            copy.wait_send()

    for copy in sends:
        copy.wait_send()


def local(coil_maps, kspace_data, interp_weights, sample_bins, spoke_count, thresholds):
    tiles, coils = lax.axis_size("tile"), lax.axis_size("coil")
    blocks = tiles * CORES
    rows, n = coil_maps.shape[1], coil_maps.shape[3]
    live = blocks * SPK_DEV // 2
    chunk = n // CHUNKS
    slot_live = jnp.arange(SPK_DEV, dtype=jnp.int32)[:, None] < spoke_count[0]
    row = jnp.where(slot_live, sample_bins // n, -1).astype(BF16)
    col = (sample_bins % n).astype(BF16)
    meta = jnp.concatenate([row[:, None], col[:, None], interp_weights], axis=1)
    meta = meta.reshape(SPK_DEV * 2, 4 * n)
    data = kspace_data[0].reshape(SPK_DEV * 2, n)
    maps = jnp.transpose(coil_maps[0], (1, 0, 2))
    consts = tables(n, LEVELS, chunk)
    vmem = pl.BlockSpec(memory_space=pltpu.VMEM)
    slots = blocks * SPK_DEV * 2
    dma = pltpu.SemaphoreType.DMA
    out = pl.pallas_call(
        functools.partial(kernel, (n, tiles, coils, rows, live)),
        out_shape=jax.ShapeDtypeStruct((2, rows, n), F32),
        in_specs=[pl.BlockSpec(memory_space=pltpu.SMEM)] + [vmem] * (3 + len(consts)),
        out_specs=vmem,
        scratch_shapes=[
            pltpu.VMEM((blocks, SPK_DEV * 2, 4 * n), BF16),
            pltpu.VMEM((blocks, SPK_DEV * 2, n), BF16),
            pltpu.VMEM((2, blocks, rows, n), F32),
            pltpu.VMEM((2, LANES, 4 * n), F32),
            pltpu.VMEM((2, LANES, n), F32),
            pltpu.VMEM((live, n, n), BF16),
            pltpu.VMEM((live, n, n), BF16),
            pltpu.VMEM((2 * n, n), BF16),
            pltpu.VMEM((2 * n, n), F32),
            pltpu.VMEM((2, n, n), BF16),
            pltpu.VMEM((2, n, n), BF16),
            pltpu.VMEM((2 * n, n), BF16),
            pltpu.VMEM((2 * n, n), BF16),
            pltpu.VMEM((2, CHUNKS, n, chunk), F32),
            pltpu.VMEM((2, CHUNKS, coils, 2, n, chunk), F32),
            pltpu.VMEM((2, CHUNKS, n, chunk), F32),
            dma((blocks,)), dma((blocks,)), dma((blocks,)), dma((blocks,)),
            dma((blocks,)), dma((blocks,)),
            dma((2, CHUNKS, coils)), dma((2, CHUNKS, coils)),
        ],
        compiler_params=pltpu.CompilerParams(
            has_side_effects=True, collective_id=0, vmem_limit_bytes=60 * 1024 * 1024
        ),
    )(thresholds, meta, data, maps, *consts)
    return jnp.transpose(out, (1, 0, 2))


def solution(mesh):
    placed = (
        P("coil", ("grp", "tile", "spk"), None, None),
        P("coil", ("grp", "tile", "spk"), None, None),
        P(("grp", "tile", "spk"), None, None),
        P(("grp", "tile", "spk"), None),
        P(("grp", "tile", "spk")),
        P(),
    )
    return jax.shard_map(
        local,
        mesh=mesh,
        in_specs=placed,
        out_specs=P(("grp", "tile", "spk"), None, None),
        check_vma=False,
    )
```

profile of v0, /device:TPU:13, one launch (start us, length us, event | category | flops | bytes accessed | tf_op | source)
XLA Modules:
  0.0 82.6 jit_solution(91031028953014552)
XLA Ops:
  0.0 0.0 copy-start.1
  0.7 0.8 fusion.6
  1.4 1.3 %reshape_squeeze.3.data_ref = bf16[16,256]{1,0:T(8,128)(2,1)} reshape(bf16[1,8,2,256]{3,2,1,0:T(2,128)(2,1)} %param.17) | data formatting | bytes 16384 | tf_op jit(solution)/shard_map/reshape;squeeze | solution.py:391
  2.7 0.0 copy-done.1
  2.8 0.0 copy-start
  2.8 0.6 reshape.8.meta_ref
  3.4 0.2 copy-done
  3.6 0.6 copy.21
  4.2 76.9 %shard_map.154 = f32[2,32,256]{2,1,0:T(8,128)} custom-call(f32[3]{0:T(128)} %thr_ref.1, bf16[16,1024]{1,0:T(8,128)(2,1)} %reshape.8.meta_ref, bf16[16,256]{1,0:T(8,128)(2,1)} %reshape_squeeze.3.data_ref, f32[2,32,256]{2,1,0:T(8,128)} %bitcast.13, bf16[256,512]{1,0:T(8,128)(2,1)} %constant.49.clone.wide_h, bf16[256,512]{1,0:T(8,128)(2,1)} %constant.50.clone.wide_l, ...), custom_call_target="tpu_custom_call" | custom-call | tf_op jit(solution)/shard_map/pallas_call | solution.py:397
  81.1 1.5 %copy.19 = f32[32,2,256]{2,1,0:T(2,128)} copy(f32[32,2,256]{2,0,1:T(8,128)} %bitcast.12) | data formatting | bytes 131072 | tf_op jit(solution)/shard_map/transpose | solution.py:427
  (3 shorter events, 0.0 us)
Async XLA Ops:
  0.0 2.8 %copy-start.1 = (bf16[8,6,256]{2,0,1:T(8,128)(2,1)S(1)}, bf16[8,6,256]{2,0,1:T(8,128)(2,1)}, u32[]{:S(2)}) copy-start(bf16[8,6,256]{2,0,1:T(8,128)(2,1)} %param.18) | copy-start | bytes 73732
  2.8 0.8 %copy-start = (f32[1,32,2,256]{3,2,1,0:T(2,128)S(1)}, f32[1,32,2,256]{3,2,1,0:T(2,128)}, u32[]{:S(2)}) copy-start(f32[1,32,2,256]{3,2,1,0:T(2,128)} %param.16) | copy-start | bytes 196612
where the time goes:
time: 83 us; the launch traced here: 82.6 us
  Pallas kernels  76.9 us (93%)
  local copies, waits for them, and re-layouts  4.29 us (5%)
    pallas_call x1, Pallas kernels, local(): pl.pallas_call(functools.partial(kernel, (n, tiles, coils, rows, live)),...  76.9 us

commit v1 on v0

v1 whole, which is shorter than its diff:
```python
import functools
import math

import jax
import jax.numpy as jnp
import numpy as np
from jax import lax
from jax.experimental import pallas as pl
from jax.experimental.pallas import tpu as pltpu
from jax.sharding import PartitionSpec as P

SPK_DEV = 8
LEVELS = 3
MEMBERS = 2**LEVELS
ITERS = 4
CORES = 2
GROUP = 2
TAPS = 3
FIELDS = 8
MARGIN = 16
STEP_SIZE = 0.5
LANES = 128
TINY = 1e-30
F32 = jnp.float32
BF16 = jnp.bfloat16
MESH = pl.DeviceIdType.MESH

_scope = [None]


def mark(name):
    if _scope[0] is not None:
        _scope[0].__exit__(None, None, None)
        _scope[0] = None
    if name:
        _scope[0] = jax.named_scope(name)
        _scope[0].__enter__()


def split_np(table):
    table = np.ascontiguousarray(table).astype(np.float32)
    high = table.astype(jnp.bfloat16)
    low = (table - high.astype(np.float32)).astype(jnp.bfloat16)
    return high, low


def haar_signs(length, levels):
    mat = np.eye(length)
    for level in range(levels):
        span = length >> level
        half = span // 2
        step = np.eye(length)
        step[:span] = 0.0
        for i in range(half):
            step[i, 2 * i] = step[i, 2 * i + 1] = 1.0
            step[half + i, 2 * i] = 1.0
            step[half + i, 2 * i + 1] = -1.0
        mat = step @ mat
    return mat


def haar_labels(length, levels):
    label = np.ones((length,), np.int32)
    for level in range(1, levels + 1):
        label = label + (np.arange(length) < length >> level)
    return label


def mirror(first, n):
    second = (n - first) % n
    second[first == 0] = n // 2
    return np.concatenate([first, second])


def orders(n):
    half = n // 2
    by_lane = mirror(np.arange(half), n)
    edge = MARGIN // 2
    near = np.concatenate([np.arange(edge), np.arange(half - edge, half), np.arange(edge, half - edge)])
    by_freq = mirror(near, n)
    groups = half // MEMBERS
    member = np.arange(half) // groups
    group = np.arange(half) % groups
    low = MEMBERS * group + member
    high = n - MEMBERS * group - member
    high[:groups] = n - MEMBERS * (np.arange(groups) + 1)
    by_pixel = np.concatenate([low, high])
    return by_lane, by_freq, low, by_pixel


def tables(n):
    half = n // 2
    by_lane, by_freq, low, by_pixel = orders(n)
    phase = np.outer(np.arange(n), np.arange(n)) % n
    angle = phase * (2.0 * np.pi / n)
    cosine = np.cos(angle) / math.sqrt(n)
    sine = np.sin(angle) / math.sqrt(n)

    def folded(outs, ins):
        bottom = sine[outs][:, ins]
        bottom[outs == 0] = cosine[half][ins]
        return np.concatenate([cosine[outs][:, ins], bottom], axis=0)

    right = folded(np.arange(half), by_lane).T
    back = folded(low, by_freq)
    fore = folded(by_freq[:half], by_pixel)
    small = haar_signs(MEMBERS, LEVELS)
    chunk_haar = []
    for q in range(2):
        pixels = by_lane[q * half : (q + 1) * half]
        mat = np.zeros((half, half))
        group = pixels // MEMBERS - q * (half // MEMBERS)
        for k in range(MEMBERS):
            mat[group * MEMBERS + k, np.arange(half)] = small[k, pixels % MEMBERS]
        both = np.kron(np.eye(2), mat)
        chunk_haar.append((both.T, both))
    haar = np.stack([np.stack(pair) for pair in chunk_haar]).astype(jnp.bfloat16)
    windows = np.stack(
        [by_freq[: half + MARGIN], np.concatenate([by_freq[half:], by_freq[:MARGIN]])]
    )
    cell_u = np.repeat(by_lane[:, None], LANES, axis=1).astype(jnp.bfloat16)
    cell_v = np.repeat(windows[:, :, None], LANES, axis=2).astype(jnp.bfloat16)
    turn_s = np.zeros((n, n))
    turn_s[np.arange(n), by_pixel] = 1.0
    turn_r = np.zeros((n, n))
    turn_r[np.arange(n), by_lane] = 1.0
    perms = np.stack([turn_s, turn_r]).astype(jnp.bfloat16)
    return (
        np.stack(split_np(right)), np.stack(split_np(back)), np.stack(split_np(fore)),
        haar, cell_u, cell_v, perms,
    )


def split(x):
    high = x.astype(BF16)
    return high, (x - high.astype(F32)).astype(BF16)


def mm(a, b):
    return jnp.dot(a, b, preferred_element_type=F32)


def mm_t(a, b):
    return lax.dot_general(a, b, (((1,), (1,)), ((), ())), preferred_element_type=F32)


def mm3(a, b):
    return mm(a[0], b[0]) + (mm(a[0], b[1]) + mm(a[1], b[0]))


def forward_haar(x):
    sums = [x[2 * i] + x[2 * i + 1] for i in range(4)]
    out = [None] * 4 + [x[2 * i] - x[2 * i + 1] for i in range(4)]
    pair = [sums[0] + sums[1], sums[2] + sums[3]]
    out[2], out[3] = sums[0] - sums[1], sums[2] - sums[3]
    out[0], out[1] = pair[0] + pair[1], pair[0] - pair[1]
    return out


def inverse_haar(c):
    pair = [c[0] + c[1], c[0] - c[1]]
    sums = [pair[0] + c[2], pair[0] - c[2], pair[1] + c[3], pair[1] - c[3]]
    out = []
    for i in range(4):
        out += [sums[i] + c[4 + i], sums[i] - c[4 + i]]
    return out


def kernel(
    dims,
    thr_ref, count_ref, weight_ref, bins_ref, data_ref, map_ref,
    right_hbm, back_hbm, fore_hbm, haar_hbm, cell_u_hbm, cell_v_hbm, perm_hbm,
    out_ref,
    right, back, fore, haar, cell_u, cell_v, perms,
    meta_mine, meta_all, data_mine, data_all, map_mine, maps,
    wide_meta, pairs, pair_data, row_tab, col_tab, kspace, grid, smeared,
    half_h, half_l, estimate, grads, sens,
    const_sem, meta_send, meta_recv, data_send, data_recv, map_send, map_recv, grad_send, grad_recv,
):
    n, tiles, coils, rows, live = dims
    half = n // 2
    window = half + MARGIN
    blocks = tiles * CORES
    slots = blocks * SPK_DEV
    pair_count = live // 2
    coil, tile, core = lax.axis_index("coil"), lax.axis_index("tile"), lax.axis_index("spk")
    pair, bit = coil // CORES, coil % CORES
    block = tile * CORES + core
    mine = pair * CORES + core

    mark("start")
    const_copies = []
    for k, (src, dst) in enumerate((
        (cell_u_hbm, cell_u), (cell_v_hbm, cell_v), (right_hbm, right), (back_hbm, back),
        (perm_hbm, perms), (haar_hbm, haar), (fore_hbm, fore),
    )):
        copy = pltpu.make_async_copy(src, dst, const_sem.at[k])
        copy.start()
        const_copies.append(copy)

    barrier = pltpu.get_barrier_semaphore()
    peers = [
        (d_bit, d_tile, d_core)
        for d_bit in range(CORES)
        for d_tile in range(tiles)
        for d_core in range(CORES)
        if d_bit + d_tile + d_core > 0
    ]
    for d_bit, d_tile, d_core in peers:
        pl.semaphore_signal(
            barrier,
            inc=1,
            device_id={
                "coil": pair * CORES + (bit + d_bit) % CORES,
                "tile": (tile + d_tile) % tiles,
                "spk": (core + d_core) % CORES,
            },
            device_id_type=MESH,
        )
    for d in range(CORES, coils):
        pl.semaphore_signal(
            barrier,
            inc=1,
            device_id={
                "coil": (coil + d // CORES * CORES) % coils,
                "spk": (core + d % CORES) % CORES,
            },
            device_id_type=MESH,
        )

    mark("prep")
    alive = lax.broadcasted_iota(jnp.int32, (SPK_DEV, n), 0) < count_ref[0]
    bins = bins_ref[...]
    row_of = jnp.where(alive, bins // n, -1).astype(F32)
    col_of = (bins % n).astype(F32)
    for j in range(0, SPK_DEV, 2):
        parts = []
        for i in (j, j + 1):
            parts += [weight_ref[i].astype(F32), row_of[i : i + 1], col_of[i : i + 1]]
        meta_mine[j * FIELDS : (j + 2) * FIELDS] = jnp.concatenate(parts, axis=0).astype(BF16)
    data_wide = data_ref[0].astype(F32)
    data_mine[...] = jnp.concatenate([data_wide[:, 0], data_wide[:, 1]], axis=0).astype(BF16)
    for p in range(2):
        map_mine[p] = map_ref[0, :, p, :]

    mark("barrier")
    pl.semaphore_wait(barrier, len(peers) + coils - CORES)

    mark("issue")
    sends = []
    for d_tile in range(tiles):
        for d_core in range(CORES):
            if d_tile == 0 and d_core == 0:
                continue
            copy = pltpu.make_async_remote_copy(
                src_ref=meta_mine,
                dst_ref=meta_all.at[block],
                send_sem=meta_send.at[d_tile * CORES + d_core],
                recv_sem=meta_recv.at[block],
                device_id={"tile": (tile + d_tile) % tiles, "spk": (core + d_core) % CORES},
                device_id_type=MESH,
            )
            copy.start()
            sends.append(copy)
    across_core = []
    for src, dst, s_sem, r_sem in (
        (data_mine, data_all.at[block], data_send, data_recv),
        (map_mine, maps.at[:, block], map_send, map_recv),
    ):
        for d_bit in range(CORES):
            for d_tile in range(tiles):
                copy = pltpu.make_async_remote_copy(
                    src_ref=src,
                    dst_ref=dst,
                    send_sem=s_sem.at[d_bit * tiles + d_tile],
                    recv_sem=r_sem.at[block],
                    device_id={
                        "coil": pair * CORES + (bit + d_bit) % CORES,
                        "tile": (tile + d_tile) % tiles,
                        "spk": bit,
                    },
                    device_id_type=MESH,
                )
                if d_bit == 0 and d_tile == 0:
                    local_copy = pltpu.make_async_copy(src, dst, r_sem.at[block])

                    @pl.when(core == bit)
                    def _(local_copy=local_copy):
                        local_copy.start()

                    @pl.when(core != bit)
                    def _(copy=copy):
                        copy.start()

                    across_core.append(copy)
                else:
                    copy.start()
                    sends.append(copy)

    mark("metawait")
    for copy in const_copies:
        copy.wait()
    meta_all[block] = meta_mine[...]
    for d_block in range(1, blocks):
        other = (block + d_block) % blocks
        pltpu.make_async_copy(meta_all.at[other], meta_all.at[other], meta_recv.at[other]).wait()

    mark("rank")
    flat = meta_all[...].reshape(slots * FIELDS, n).astype(F32)
    for t in range(n // LANES):
        wide_meta[t] = flat[:, t * LANES : (t + 1) * LANES]

    def field(m):
        return jnp.concatenate(
            [wide_meta[t, pl.ds(m, slots, stride=FIELDS), :] for t in range(n // LANES)], axis=1
        )

    rows_all = field(2 * TAPS)
    up = lax.broadcasted_iota(jnp.int32, (slots, slots), 0)
    across = lax.broadcasted_iota(jnp.int32, (slots, slots), 1)
    flag = jnp.where(rows_all[:, :LANES] >= 0.0, 1.0 / LANES, 0.0)
    flags = mm_t(jnp.ones((live, LANES), BF16), flag.astype(BF16)).astype(BF16)
    rank = mm(flags, jnp.where(up < across, 1.0, 0.0).astype(BF16))
    here = lax.broadcasted_iota(jnp.int32, (live, slots), 0).astype(F32)
    hit = (flags.astype(F32) > 0.5) & (rank == here)
    pick = jnp.where(hit, 1.0, 0.0).astype(BF16)
    comp = [mm(pick, (rows_all if m == 2 * TAPS else field(m)).astype(BF16)) for m in range(FIELDS)]
    first_low = jnp.broadcast_to(comp[2 * TAPS + 1][:, 1:2], (live, half)) < half

    def halves(x):
        low = jnp.where(first_low, x[:, :half], x[:, half:])
        high = jnp.where(first_low, x[:, half:], x[:, :half])
        return [jnp.concatenate([v[:pair_count], v[pair_count:]], axis=1) for v in (low, high)]

    for m in range(2 * TAPS):
        for o, value in enumerate(halves(comp[m])):
            pairs[o, m] = value
    for m, centre in ((2 * TAPS, comp[2 * TAPS]), (3 * TAPS, comp[2 * TAPS + 1])):
        for t in range(TAPS):
            tap = (centre.astype(jnp.int32) + (t - 1)) & (n - 1)
            for o, value in enumerate(halves(tap.astype(F32))):
                pairs[o, m + t] = value

    mark("build")

    def build(i, carry):
        def table(cells, m, o):
            def part(k):
                return jnp.broadcast_to(pairs[o, k, pl.ds(i, 1), :].astype(BF16), cells.shape)

            zero = jnp.zeros(cells.shape, BF16)
            return jnp.where(
                cells == part(2 * TAPS + m), part(m),
                jnp.where(
                    cells == part(2 * TAPS + m + 1), part(m + 1),
                    jnp.where(cells == part(2 * TAPS + m + 2), part(m + 2), zero),
                ),
            )

        for o in range(2):
            cells = jnp.concatenate([cell_u[...]] * (n // LANES), axis=1)
            row_tab[i, o] = table(cells, 0, o)
            cells = jnp.concatenate([cell_v[o]] * (n // LANES), axis=1)
            col_tab[i, o] = table(cells, TAPS, o)
        return carry

    lax.fori_loop(0, pair_count, build, 0)

    mark("datawait")
    for b in range(blocks):
        pltpu.make_async_copy(data_all.at[b], data_all.at[b], data_recv.at[b]).wait()
    offset = jnp.abs(lax.broadcasted_iota(jnp.int32, (live, n), 1) - half).astype(F32)
    density = (offset + 0.5) * (n / (3.0 * n * live))
    for o, value in enumerate(halves(density)):
        pair_data[o, 2] = value
    every = data_all[...]
    for p in range(2):
        samples = jnp.concatenate(
            [every[b].astype(F32)[p * SPK_DEV : (p + 1) * SPK_DEV] for b in range(blocks)], axis=0
        )
        for o, value in enumerate(halves(mm(pick, samples.astype(BF16)))):
            pair_data[o, p] = value

    first_lane = lax.broadcasted_iota(jnp.int32, (n, half), 1) == 0
    first_row = lax.broadcasted_iota(jnp.int32, (half, half), 0) == 0
    groups = half // MEMBERS
    label = haar_labels(MEMBERS, LEVELS)
    lane = lax.broadcasted_iota(jnp.int32, (1, half), 1) % MEMBERS
    lane_label = jnp.ones((1, half), jnp.int32)
    for level in range(1, LEVELS + 1):
        lane_label = lane_label + jnp.where(lane < MEMBERS >> level, 1, 0)

    def norm_of(k):
        return 1.0 / math.sqrt((haar_signs(MEMBERS, LEVELS)[k] ** 2).sum())

    lane_norm = jnp.zeros((1, half), F32)
    for k in range(MEMBERS):
        lane_norm = jnp.where(lane == k, norm_of(k), lane_norm)
    limits, scales = [], []
    for k in range(MEMBERS):
        band = jnp.minimum(lane_label, int(label[k]))
        limit = jnp.zeros((1, half), F32)
        for level in range(LEVELS):
            limit = jnp.where(band == level + 1, thr_ref[level], limit)
        limits.append(limit)
        scales.append(lane_norm * norm_of(k))

    for it in range(ITERS):
        slot = it % 2
        mark("spokes")
        grid[...] = jnp.zeros_like(grid)

        def fore_step(step, into, it=it):
            for g in range(GROUP):
                i = step * GROUP + g
                for o in range(2):
                    col = col_tab[i, o].astype(F32)
                    dens = pair_data[o, 2, pl.ds(i, 1), :]
                    inner = mm(kspace[o], row_tab[i, o]) if it > 0 else None
                    for p in range(2):
                        value = -pair_data[o, p, pl.ds(i, 1), :]
                        if it > 0:
                            value = value + jnp.sum(
                                inner[p * window : (p + 1) * window] * col, axis=0, keepdims=True
                            )
                        smeared[into, o, p * window : (p + 1) * window, g * n : (g + 1) * n] = (
                            col * (dens * value)
                        ).astype(BF16)

        def back_step(step, source):
            for o in range(2):
                total = None
                for g in range(GROUP):
                    added = mm_t(
                        smeared[source, o, :, g * n : (g + 1) * n], row_tab[step * GROUP + g, o]
                    )
                    total = added if total is None else total + added
                grid[o] += total

        steps = pair_count // GROUP
        fore_step(0, 0)

        def body(step, carry):
            into = step % 2
            fore_step(step, into)
            back_step(step - 1, 1 - into)
            return carry

        lax.fori_loop(1, steps, body, 0)
        back_step(steps - 1, (steps - 1) % 2)

        mark("turned")
        stack = []
        for p in range(2):
            low, high = grid[0, p * window : (p + 1) * window], grid[1, p * window : (p + 1) * window]
            stack += [
                low[:MARGIN] + high[half:], low[MARGIN:half],
                high[:MARGIN] + low[half:], high[MARGIN:half],
            ]
        turned = mm3(split(jnp.concatenate(stack, axis=0)), (right[0], right[1]))
        r_c, i_c = turned[:n, :half], turned[n:, :half]
        r_s, i_s = turned[:n, half:], turned[n:, half:]
        r_z, i_z = jnp.where(first_lane, 0.0, r_s), jnp.where(first_lane, 0.0, i_s)
        sides = [
            split(jnp.concatenate([r_c - i_z, i_c + r_z], axis=1)),
            split(jnp.concatenate(
                [jnp.where(first_lane, r_s, r_c + i_s), jnp.where(first_lane, i_s, i_c - r_s)], axis=1
            )),
        ]
        if it == 0:
            mark("mapwait")
            for b in range(blocks):
                pltpu.make_async_copy(maps.at[:, b], maps.at[:, b], map_recv.at[b]).wait()
            for p in range(2):
                plain = split(maps[p].reshape(n, n))
                moved = split(sum(mm(perms[1], x) for x in plain))
                both = sum(mm_t(perms[0], x) for x in moved)
                for q in range(2):
                    sens[p, q] = both[:, q * half : (q + 1) * half]

        mark("image")
        copies = []
        for q in range(2):
            w = mm3((back[0], back[1]), sides[q])
            c_r, c_i, s_r, s_i = w[:half, :half], w[:half, half:], w[half:, :half], w[half:, half:]
            z_r, z_i = jnp.where(first_row, 0.0, s_r), jnp.where(first_row, 0.0, s_i)
            low_r, low_i = c_r - z_i, c_i + z_r
            high_r = jnp.where(first_row, s_r, c_r + s_i)
            high_i = jnp.where(first_row, s_i, c_i - s_r)
            d_r = jnp.concatenate(
                [low_r, pltpu.roll(high_r[:groups], groups - 1, 0), high_r[groups:]], axis=0
            )
            d_i = jnp.concatenate(
                [low_i, pltpu.roll(high_i[:groups], groups - 1, 0), high_i[groups:]], axis=0
            )
            m_r, m_i = sens[0, q], sens[1, q]
            grads[slot, q, mine, 0] = m_r * d_r + m_i * d_i
            grads[slot, q, mine, 1] = m_r * d_i - m_i * d_r
            for d in range(1, coils):
                d_pair, d_core = d // CORES, d % CORES
                copy = pltpu.make_async_remote_copy(
                    src_ref=grads.at[slot, q, mine],
                    dst_ref=grads.at[slot, q, mine],
                    send_sem=grad_send.at[slot, q, d],
                    recv_sem=grad_recv.at[slot, q, mine],
                    device_id={
                        "coil": (coil + d_pair * CORES) % coils,
                        "spk": (core + d_core) % CORES,
                    },
                    device_id_type=MESH,
                )
                copy.start()
                copies.append(copy)

        for q in range(2):
            mark("gradwait")
            for d in range(1, coils):
                d_pair, d_core = d // CORES, d % CORES
                other = (coil + d_pair * CORES) % coils // CORES * CORES + (core + d_core) % CORES
                pltpu.make_async_copy(
                    grads.at[slot, q, other], grads.at[slot, q, other], grad_recv.at[slot, q, other]
                ).wait()
            mark("shrink")
            summed = grads[slot, q, 0]
            for c in range(1, coils):
                summed = summed + grads[slot, q, c]
            target = -STEP_SIZE * jnp.concatenate([summed[0], summed[1]], axis=1)
            if it > 0:
                target = estimate[q] + target

            def piece(x, h, m):
                first = h * half + (m if h == 0 else (MEMBERS - m) % MEMBERS) * groups
                return x[first : first + groups]

            along = []
            for h in range(2):
                along += forward_haar([piece(target, h, m) for m in range(MEMBERS)])
            side = split(jnp.concatenate(along, axis=0))
            coeffs = mm(side[0], haar[q, 0]) + mm(side[1], haar[q, 0])
            shrunk = []
            for h in range(2):
                for k in range(MEMBERS):
                    first = h * half + k * groups
                    c_r = coeffs[first : first + groups, :half] * scales[k]
                    c_i = coeffs[first : first + groups, half:] * scales[k]
                    power = jnp.maximum(c_r * c_r + c_i * c_i, TINY)
                    factor = jnp.maximum(1.0 - limits[k] * lax.rsqrt(power), 0.0) * scales[k]
                    shrunk.append(jnp.concatenate([c_r * factor, c_i * factor], axis=1))
            side = split(jnp.concatenate(shrunk, axis=0))
            along = mm(side[0], haar[q, 1]) + mm(side[1], haar[q, 1])
            fresh = []
            for h in range(2):
                first = h * half
                members = inverse_haar(
                    [along[first + k * groups : first + (k + 1) * groups] for k in range(MEMBERS)]
                )
                placed = [None] * MEMBERS
                for m in range(MEMBERS):
                    placed[m if h == 0 else (MEMBERS - m) % MEMBERS] = members[m]
                fresh += placed
            fresh = jnp.concatenate(fresh, axis=0)
            estimate[q] = fresh
            if it < ITERS - 1:
                mark("fwd")
                e_r, e_i = fresh[:, :half], fresh[:, half:]
                m_r, m_i = sens[0, q], sens[1, q]
                seen = split(
                    jnp.concatenate([m_r * e_r - m_i * e_i, m_r * e_i + m_i * e_r], axis=1)
                )
                w = mm3((fore[0], fore[1]), seen)
                c_r, c_i, s_r, s_i = w[:half, :half], w[:half, half:], w[half:, :half], w[half:, half:]
                z_r, z_i = jnp.where(first_row, 0.0, s_r), jnp.where(first_row, 0.0, s_i)
                v = jnp.concatenate(
                    [
                        c_r + z_i, jnp.where(first_row, s_r, c_r - s_i),
                        c_i - z_r, jnp.where(first_row, s_i, c_i + s_r),
                    ],
                    axis=0,
                )
                half_h[:, q * half : (q + 1) * half], half_l[:, q * half : (q + 1) * half] = split(v)
        mark("sendwait")
        for copy in copies:
            copy.wait_send()
        if it < ITERS - 1:
            mark("vfft")
            v = mm3((half_h[...], half_l[...]), (right[0], right[1]))
            r_c, i_c, r_s, i_s = v[:n, :half], v[n:, :half], v[:n, half:], v[n:, half:]
            r_z, i_z = jnp.where(first_lane, 0.0, r_s), jnp.where(first_lane, 0.0, i_s)
            whole = [
                jnp.concatenate([r_c + i_z, jnp.where(first_lane, r_s, r_c - i_s)], axis=1).astype(BF16),
                jnp.concatenate([i_c - r_z, jnp.where(first_lane, i_s, i_c + r_s)], axis=1).astype(BF16),
            ]
            for p in range(2):
                first = p * window
                kspace[0, first : first + window] = whole[p][:window]
                kspace[1, first : first + half] = whole[p][half:]
                kspace[1, first + half : first + window] = whole[p][:MARGIN]

    mark("out")
    take = lax.broadcasted_iota(jnp.int32, (rows, n), 0) + block * rows
    at = lax.broadcasted_iota(jnp.int32, (rows, n), 1)
    owner = jnp.where(at <= half, at, n + half - at)
    chosen = jnp.where(take == owner, 1.0, 0.0).astype(BF16)
    for p in range(2):
        mine_rows = jnp.concatenate([estimate[q, :, p * half : (p + 1) * half] for q in range(2)], axis=1)
        picked = sum(mm_t(chosen, x) for x in split(mine_rows))
        out_ref[:, p, :] = sum(mm(x, perms[0]) for x in split(picked))

    @pl.when(core != bit)
    def _():
        for copy in across_core:
            copy.wait_send()

    for copy in sends:
        copy.wait_send()
    mark(None)


def local(coil_maps, kspace_data, interp_weights, sample_bins, spoke_count, thresholds):
    tiles, coils = lax.axis_size("tile"), lax.axis_size("coil")
    blocks = tiles * CORES
    rows, n = coil_maps.shape[1], coil_maps.shape[3]
    live = blocks * SPK_DEV // 2
    half = n // 2
    window = half + MARGIN
    consts = tables(n)
    vmem = pl.BlockSpec(memory_space=pltpu.VMEM)
    smem = pl.BlockSpec(memory_space=pltpu.SMEM)
    slots = blocks * SPK_DEV
    pair_count = live // 2
    dma = pltpu.SemaphoreType.DMA
    return pl.pallas_call(
        functools.partial(kernel, (n, tiles, coils, rows, live)),
        out_shape=jax.ShapeDtypeStruct((rows, 2, n), F32),
        in_specs=[smem, smem] + [vmem] * 4 + [pl.BlockSpec(memory_space=pl.ANY)] * len(consts),
        out_specs=vmem,
        scratch_shapes=[pltpu.VMEM(c.shape, BF16) for c in consts] + [
            pltpu.VMEM((SPK_DEV * FIELDS, n), BF16),
            pltpu.VMEM((blocks, SPK_DEV * FIELDS, n), BF16),
            pltpu.VMEM((SPK_DEV * 2, n), BF16),
            pltpu.VMEM((blocks, SPK_DEV * 2, n), BF16),
            pltpu.VMEM((2, rows, n), F32),
            pltpu.VMEM((2, blocks, rows, n), F32),
            pltpu.VMEM((n // LANES, slots * FIELDS, LANES), F32),
            pltpu.VMEM((2, 4 * TAPS, pair_count, n), F32),
            pltpu.VMEM((2, 3, pair_count, n), F32),
            pltpu.VMEM((pair_count, 2, n, n), BF16),
            pltpu.VMEM((pair_count, 2, window, n), BF16),
            pltpu.VMEM((2, 2 * window, n), BF16),
            pltpu.VMEM((2, 2 * window, n), F32),
            pltpu.VMEM((2, 2, 2 * window, GROUP * n), BF16),
            pltpu.VMEM((2 * n, n), BF16),
            pltpu.VMEM((2 * n, n), BF16),
            pltpu.VMEM((2, n, n), F32),
            pltpu.VMEM((2, 2, coils, 2, n, half), F32),
            pltpu.VMEM((2, 2, n, half), F32),
            dma((len(consts),)),
            dma((blocks,)), dma((blocks,)), dma((blocks,)), dma((blocks,)),
            dma((blocks,)), dma((blocks,)),
            dma((2, 2, coils)), dma((2, 2, coils)),
        ],
        compiler_params=pltpu.CompilerParams(
            has_side_effects=True, collective_id=0, vmem_limit_bytes=60 * 1024 * 1024
        ),
    )(thresholds, spoke_count, interp_weights, sample_bins, kspace_data, coil_maps, *consts)


def solution(mesh):
    placed = (
        P("coil", ("grp", "tile", "spk"), None, None),
        P("coil", ("grp", "tile", "spk"), None, None),
        P(("grp", "tile", "spk"), None, None),
        P(("grp", "tile", "spk"), None),
        P(("grp", "tile", "spk")),
        P(),
    )
    return jax.shard_map(
        local,
        mesh=mesh,
        in_specs=placed,
        out_specs=P(("grp", "tile", "spk"), None, None),
        check_vma=False,
    )
```

time: 83 us -> 63.2 us (0.76)
  the two profiles are of different devices: /device:TPU:13 before, /device:TPU:1 now
where the time goes in v1:
time: 63.2 us; the launch traced here: 62.9 us
  Pallas kernels  59.4 us (94%)
  local copies, waits for them, and re-layouts  2.83 us (4%)
  between operations  0.66 us (1%)
    pallas_call x1, Pallas kernels, local(): pl.pallas_call(functools.partial(kernel, (n, tiles, coils, rows, live)),...  59.4 us
    unnamed x2, local copies, waits for them, and re-layouts  2.83 us

profile of v1, /device:TPU:1, one launch (start us, length us, event | category | flops | bytes accessed | tf_op | source)
XLA Modules:
  0.0 62.9 jit_solution(13017749847053723085)
XLA Ops:
  0.7 1.4 %copy.14.weight_ref = bf16[8,6,256]{2,1,0:T(8,128)(2,1)} copy(bf16[8,6,256]{2,0,1:T(8,128)(2,1)} %param.15) | data formatting | bytes 49152 | tf_op args[2]
  2.0 59.4 %shard_map.127 = f32[32,2,256]{2,1,0:T(2,128)} custom-call(f32[3]{0:T(128)} %thr_ref.1, s32[1]{0:T(128)S(6)} %copy.16.count_ref, bf16[8,6,256]{2,1,0:T(8,128)(2,1)} %copy.14.weight_ref, s32[8,256]{1,0:T(8,128)} %bins_ref.1, bf16[1,8,2,256]{3,2,1,0:T(2,128)(2,1)} %data_ref.1, f32[1,32,2,256]{3,2,1,0:T(2,128)} %map_ref.1, ...), custom_call_target="tpu_custom_call" | custom-call | tf_op jit(solution)/shard_map/pallas_call | solution.py:632
  61.4 1.5 %copy.17 = f32[32,2,256]{2,1,0:T(2,128)} copy(f32[32,2,256]{2,1,0:T(2,128)} %shard_map.127) | data formatting | bytes 131072

commit v2 on v1

--- a/solution.py
+++ b/solution.py
@@ -21,6 +21,7 @@
 STEP_SIZE = 0.5
 LANES = 128
 TINY = 1e-30
+VMEM_LIMIT = 60 * 1024 * 1024
 F32 = jnp.float32
 BF16 = jnp.bfloat16
 MESH = pl.DeviceIdType.MESH
@@ -168,14 +169,14 @@
 
 def kernel(
     dims,
-    thr_ref, count_ref, weight_ref, bins_ref, data_ref, map_ref,
+    thr_ref, count_ref, weight_hbm, bins_hbm, data_hbm, map_hbm,
     right_hbm, back_hbm, fore_hbm, haar_hbm, cell_u_hbm, cell_v_hbm, perm_hbm,
     out_ref,
     right, back, fore, haar, cell_u, cell_v, perms,
-    meta_mine, meta_all, data_mine, data_all, map_mine, maps,
-    wide_meta, pairs, pair_data, row_tab, col_tab, kspace, grid, smeared,
+    bins_ref, data_ref, map_ref, meta_mine, meta_all, data_mine, data_all, map_mine, maps,
+    pairs, pair_data, row_tab, col_tab, kspace, grid, smear_a, smear_b,
     half_h, half_l, estimate, grads, sens,
-    const_sem, meta_send, meta_recv, data_send, data_recv, map_send, map_recv, grad_send, grad_recv,
+    const_sem, arg_sem, meta_send, meta_recv, data_send, data_recv, map_send, map_recv, grad_send, grad_recv,
 ):
     n, tiles, coils, rows, live = dims
     half = n // 2
@@ -188,23 +189,22 @@
     block = tile * CORES + core
     mine = pair * CORES + core
 
+    def toggled(value, d):
+        step = 1
+        while step <= d:
+            if d & step:
+                value = value + step - 2 * step * (value // step % 2)
+            step *= 2
+        return value
+
     mark("start")
-    const_copies = []
-    for k, (src, dst) in enumerate((
-        (cell_u_hbm, cell_u), (cell_v_hbm, cell_v), (right_hbm, right), (back_hbm, back),
-        (perm_hbm, perms), (haar_hbm, haar), (fore_hbm, fore),
-    )):
-        copy = pltpu.make_async_copy(src, dst, const_sem.at[k])
-        copy.start()
-        const_copies.append(copy)
-
     barrier = pltpu.get_barrier_semaphore()
     peers = [
         (d_bit, d_tile, d_core)
         for d_bit in range(CORES)
         for d_tile in range(tiles)
         for d_core in range(CORES)
-        if d_bit + d_tile + d_core > 0
+        if (d_tile > 0 and d_bit == 0) or (d_tile < 2 and d_tile + d_bit + d_core > 0)
     ]
     for d_bit, d_tile, d_core in peers:
         pl.semaphore_signal(
@@ -212,7 +212,7 @@
             inc=1,
             device_id={
                 "coil": pair * CORES + (bit + d_bit) % CORES,
-                "tile": (tile + d_tile) % tiles,
+                "tile": toggled(tile, d_tile),
                 "spk": (core + d_core) % CORES,
             },
             device_id_type=MESH,
@@ -227,93 +227,145 @@
             },
             device_id_type=MESH,
         )
+    arg_copies = []
+    for k, (src, dst) in enumerate((
+        (bins_hbm, bins_ref), (weight_hbm, meta_mine.at[: 2 * TAPS]),
+        (data_hbm, data_ref), (map_hbm, map_ref),
+    )):
+        copy = pltpu.make_async_copy(src, dst, arg_sem.at[k])
+        copy.start()
+        arg_copies.append(copy)
+    const_copies = []
+    for k, (src, dst) in enumerate((
+        (perm_hbm, perms), (cell_u_hbm, cell_u), (cell_v_hbm, cell_v), (right_hbm, right),
+        (back_hbm, back), (haar_hbm, haar), (fore_hbm, fore),
+    )):
+        copy = pltpu.make_async_copy(src, dst, const_sem.at[k])
+        copy.start()
+        const_copies.append(copy)
 
     mark("prep")
+    for copy in arg_copies:
+        copy.wait()
     alive = lax.broadcasted_iota(jnp.int32, (SPK_DEV, n), 0) < count_ref[0]
     bins = bins_ref[...]
     row_of = jnp.where(alive, bins // n, -1).astype(F32)
     col_of = (bins % n).astype(F32)
-    for j in range(0, SPK_DEV, 2):
-        parts = []
-        for i in (j, j + 1):
-            parts += [weight_ref[i].astype(F32), row_of[i : i + 1], col_of[i : i + 1]]
-        meta_mine[j * FIELDS : (j + 2) * FIELDS] = jnp.concatenate(parts, axis=0).astype(BF16)
+    meta_mine[2 * TAPS] = row_of.astype(BF16)
+    meta_mine[2 * TAPS + 1] = col_of.astype(BF16)
     data_wide = data_ref[0].astype(F32)
     data_mine[...] = jnp.concatenate([data_wide[:, 0], data_wide[:, 1]], axis=0).astype(BF16)
-    for p in range(2):
-        map_mine[p] = map_ref[0, :, p, :]
-
     mark("barrier")
     pl.semaphore_wait(barrier, len(peers) + coils - CORES)
 
     mark("issue")
     sends = []
-    for d_tile in range(tiles):
-        for d_core in range(CORES):
-            if d_tile == 0 and d_core == 0:
-                continue
-            copy = pltpu.make_async_remote_copy(
-                src_ref=meta_mine,
-                dst_ref=meta_all.at[block],
-                send_sem=meta_send.at[d_tile * CORES + d_core],
-                recv_sem=meta_recv.at[block],
-                device_id={"tile": (tile + d_tile) % tiles, "spk": (core + d_core) % CORES},
-                device_id_type=MESH,
-            )
-            copy.start()
-            sends.append(copy)
-    across_core = []
-    for src, dst, s_sem, r_sem in (
-        (data_mine, data_all.at[block], data_send, data_recv),
-        (map_mine, maps.at[:, block], map_send, map_recv),
-    ):
-        for d_bit in range(CORES):
-            for d_tile in range(tiles):
-                copy = pltpu.make_async_remote_copy(
-                    src_ref=src,
-                    dst_ref=dst,
-                    send_sem=s_sem.at[d_bit * tiles + d_tile],
-                    recv_sem=r_sem.at[block],
-                    device_id={
-                        "coil": pair * CORES + (bit + d_bit) % CORES,
-                        "tile": (tile + d_tile) % tiles,
-                        "spk": bit,
-                    },
-                    device_id_type=MESH,
-                )
-                if d_bit == 0 and d_tile == 0:
-                    local_copy = pltpu.make_async_copy(src, dst, r_sem.at[block])
-
-                    @pl.when(core == bit)
-                    def _(local_copy=local_copy):
-                        local_copy.start()
-
-                    @pl.when(core != bit)
-                    def _(copy=copy):
-                        copy.start()
-
-                    across_core.append(copy)
-                else:
-                    copy.start()
-                    sends.append(copy)
+    near = [toggled(tile, d) for d in range(tiles)]
+    far_first = list(range(tiles // 2, tiles)) + list(range(1, tiles // 2))
+
+    def send(src, dst, s_sem, r_sem, target):
+        copy = pltpu.make_async_remote_copy(
+            src_ref=src, dst_ref=dst, send_sem=s_sem, recv_sem=r_sem,
+            device_id=target, device_id_type=MESH,
+        )
+        copy.start()
+        return copy
+
+    for d in far_first:
+        sends.append(send(
+            meta_mine, meta_all.at[block], meta_send.at[d], meta_recv.at[block], {"tile": near[d]}
+        ))
+    sends.append(send(
+        meta_mine, meta_all.at[block], meta_send.at[0], meta_recv.at[block], {"spk": 1 - core}
+    ))
+    inner = []
+    across = pair * CORES + 1 - bit
+    routes = [{"coil": across, "spk": bit}, {"tile": near[1], "spk": bit},
+              {"coil": across, "tile": near[1], "spk": bit}]
+    routes += [{"tile": near[d], "spk": bit} for d in far_first if d > 1]
+
+    def spread(src, dst, s_sem, r_sem):
+        for k, route in enumerate(routes):
+            sends.append(send(src, dst, s_sem.at[1 + k], r_sem, route))
+        local_copy = pltpu.make_async_copy(src, dst, r_sem)
+        inner_copy = pltpu.make_async_remote_copy(
+            src_ref=src, dst_ref=dst, send_sem=s_sem.at[0], recv_sem=r_sem,
+            device_id={"spk": 1 - core}, device_id_type=MESH,
+        )
+        inner.append(inner_copy)
+
+        @pl.when(core == bit)
+        def _():
+            local_copy.start()
+
+        @pl.when(core != bit)
+        def _():
+            inner_copy.start()
+
+    spread(data_mine, data_all.at[block], data_send, data_recv.at[block])
+    const_copies[0].wait()
+    for p in range(2):
+        map_mine[p] = sum(mm_t(x, perms[0]) for x in split(map_ref[0, :, p, :]))
+    spread(map_mine, maps.at[:, block], map_send, map_recv.at[block])
+
+    def arrived(ref, sem):
+        pltpu.make_async_copy(ref, ref, sem).wait()
+
+    def hand_over(ref, s_sem, r_sem):
+        return (
+            pltpu.make_async_copy(ref, ref, r_sem),
+            pltpu.make_async_remote_copy(
+                src_ref=ref, dst_ref=ref, send_sem=s_sem, recv_sem=r_sem,
+                device_id={"coil": across}, device_id_type=MESH,
+            ),
+        )
+
+    map_hand, data_hand = [], []
+    for d in far_first:
+        if d < 2:
+            continue
+        for c in range(CORES):
+            b = near[d] * CORES + c
+            k = 2 + tiles + len(map_hand)
+            map_hand.append(hand_over(maps.at[:, b], map_send.at[k], map_recv.at[b]))
+            data_hand.append(hand_over(data_all.at[b], data_send.at[k], data_recv.at[b]))
+
+    def pass_on(hands):
+        @pl.when(core == bit)
+        def _():
+            for here, there in hands:
+                here.wait()
+                there.start()
 
     mark("metawait")
-    for copy in const_copies:
+    for copy in const_copies[1:]:
         copy.wait()
     meta_all[block] = meta_mine[...]
-    for d_block in range(1, blocks):
-        other = (block + d_block) % blocks
-        pltpu.make_async_copy(meta_all.at[other], meta_all.at[other], meta_recv.at[other]).wait()
+    for d in range(1, tiles):
+        b = near[d] * CORES + core
+        arrived(meta_all.at[b], meta_recv.at[b])
+        sends.append(send(
+            meta_all.at[b], meta_all.at[b], meta_send.at[tiles + d], meta_recv.at[b], {"spk": 1 - core}
+        ))
+    for d in range(tiles):
+        b = near[d] * CORES + 1 - core
+        arrived(meta_all.at[b], meta_recv.at[b])
+
+    mark("pass")
+
+    pass_on(data_hand)
+    direct = [near[d] * CORES + c for d in range(2) for c in range(CORES)]
+
+    @pl.when(core == bit)
+    def _():
+        for b in direct:
+            arrived(data_all.at[b], data_recv.at[b])
 
     mark("rank")
-    flat = meta_all[...].reshape(slots * FIELDS, n).astype(F32)
-    for t in range(n // LANES):
-        wide_meta[t] = flat[:, t * LANES : (t + 1) * LANES]
+    whole = [meta_all[b].reshape(FIELDS * SPK_DEV, n).astype(F32) for b in range(blocks)]
 
     def field(m):
-        return jnp.concatenate(
-            [wide_meta[t, pl.ds(m, slots, stride=FIELDS), :] for t in range(n // LANES)], axis=1
-        )
+        return jnp.concatenate([w[m * SPK_DEV : (m + 1) * SPK_DEV] for w in whole], axis=0)
 
     rows_all = field(2 * TAPS)
     up = lax.broadcasted_iota(jnp.int32, (slots, slots), 0)
@@ -341,6 +393,8 @@
             for o, value in enumerate(halves(tap.astype(F32))):
                 pairs[o, m + t] = value
 
+    stage = len(map_hand) // 2
+    pass_on(map_hand[:stage])
     mark("build")
 
     def build(i, carry):
@@ -367,8 +421,13 @@
     lax.fori_loop(0, pair_count, build, 0)
 
     mark("datawait")
-    for b in range(blocks):
-        pltpu.make_async_copy(data_all.at[b], data_all.at[b], data_recv.at[b]).wait()
+    pass_on(map_hand[stage:])
+
+    @pl.when(core != bit)
+    def _():
+        for b in range(blocks):
+            arrived(data_all.at[b], data_recv.at[b])
+
     offset = jnp.abs(lax.broadcasted_iota(jnp.int32, (live, n), 1) - half).astype(F32)
     density = (offset + 0.5) * (n / (3.0 * n * live))
     for o, value in enumerate(halves(density)):
@@ -405,6 +464,7 @@
         limits.append(limit)
         scales.append(lane_norm * norm_of(k))
 
+    copies = []
     for it in range(ITERS):
         slot = it % 2
         mark("spokes")
@@ -416,14 +476,14 @@
                 for o in range(2):
                     col = col_tab[i, o].astype(F32)
                     dens = pair_data[o, 2, pl.ds(i, 1), :]
-                    inner = mm(kspace[o], row_tab[i, o]) if it > 0 else None
+                    seen = mm(kspace[o], row_tab[i, o]) if it > 0 else None
                     for p in range(2):
                         value = -pair_data[o, p, pl.ds(i, 1), :]
                         if it > 0:
                             value = value + jnp.sum(
-                                inner[p * window : (p + 1) * window] * col, axis=0, keepdims=True
+                                seen[p * window : (p + 1) * window] * col, axis=0, keepdims=True
                             )
-                        smeared[into, o, p * window : (p + 1) * window, g * n : (g + 1) * n] = (
+                        into[o, p * window : (p + 1) * window, g * n : (g + 1) * n] = (
                             col * (dens * value)
                         ).astype(BF16)
 
@@ -432,22 +492,28 @@
                 total = None
                 for g in range(GROUP):
                     added = mm_t(
-                        smeared[source, o, :, g * n : (g + 1) * n], row_tab[step * GROUP + g, o]
+                        source[o, :, g * n : (g + 1) * n], row_tab[step * GROUP + g, o]
                     )
                     total = added if total is None else total + added
                 grid[o] += total
 
-        steps = pair_count // GROUP
-        fore_step(0, 0)
-
-        def body(step, carry):
-            into = step % 2
-            fore_step(step, into)
-            back_step(step - 1, 1 - into)
+        turns = pair_count // GROUP // 2
+        fore_step(0, smear_a)
+
+        def body(turn, carry):
+            back_step(2 * turn, smear_a)
+            fore_step(2 * turn + 1, smear_b)
+            back_step(2 * turn + 1, smear_b)
+            fore_step(2 * turn + 2, smear_a)
             return carry
 
-        lax.fori_loop(1, steps, body, 0)
-        back_step(steps - 1, (steps - 1) % 2)
+        lax.fori_loop(0, turns - 1, body, 0)
+        back_step(2 * turns - 2, smear_a)
+        fore_step(2 * turns - 1, smear_b)
+        back_step(2 * turns - 1, smear_b)
+
+        for copy in copies:
+            copy.wait_send()
 
         mark("turned")
         stack = []
@@ -469,12 +535,24 @@
         ]
         if it == 0:
             mark("mapwait")
-            for b in range(blocks):
-                pltpu.make_async_copy(maps.at[:, b], maps.at[:, b], map_recv.at[b]).wait()
+
+            @pl.when(core != bit)
+            def _():
+                for b in range(blocks):
+                    arrived(maps.at[:, b], map_recv.at[b])
+
+            @pl.when(core == bit)
+            def _():
+                for b in direct:
+                    arrived(maps.at[:, b], map_recv.at[b])
+
             for p in range(2):
-                plain = split(maps[p].reshape(n, n))
-                moved = split(sum(mm(perms[1], x) for x in plain))
-                both = sum(mm_t(perms[0], x) for x in moved)
+                both = sum(
+                    lax.dot_general(
+                        x, perms[1], (((0,), (1,)), ((), ())), preferred_element_type=F32
+                    )
+                    for x in split(maps[p].reshape(n, n))
+                )
                 for q in range(2):
                     sens[p, q] = both[:, q * half : (q + 1) * half]
 
@@ -512,6 +590,7 @@
                 copy.start()
                 copies.append(copy)
 
+        coeff_of = []
         for q in range(2):
             mark("gradwait")
             for d in range(1, coils):
@@ -536,7 +615,9 @@
             for h in range(2):
                 along += forward_haar([piece(target, h, m) for m in range(MEMBERS)])
             side = split(jnp.concatenate(along, axis=0))
-            coeffs = mm(side[0], haar[q, 0]) + mm(side[1], haar[q, 0])
+            coeff_of.append(mm(side[0], haar[q, 0]) + mm(side[1], haar[q, 0]))
+        for q in range(2):
+            coeffs = coeff_of[q]
             shrunk = []
             for h in range(2):
                 for k in range(MEMBERS):
@@ -578,9 +659,6 @@
                     axis=0,
                 )
                 half_h[:, q * half : (q + 1) * half], half_l[:, q * half : (q + 1) * half] = split(v)
-        mark("sendwait")
-        for copy in copies:
-            copy.wait_send()
         if it < ITERS - 1:
             mark("vfft")
             v = mm3((half_h[...], half_l[...]), (right[0], right[1]))
@@ -604,14 +682,21 @@
     for p in range(2):
         mine_rows = jnp.concatenate([estimate[q, :, p * half : (p + 1) * half] for q in range(2)], axis=1)
         picked = sum(mm_t(chosen, x) for x in split(mine_rows))
-        out_ref[:, p, :] = sum(mm(x, perms[0]) for x in split(picked))
+        result = sum(mm(x, perms[0]) for x in split(picked))
+        for t in range(n // LANES):
+            out_ref[pl.ds(t * 2 + p, rows, stride=2 * n // LANES), :] = result[:, t * LANES : (t + 1) * LANES]
 
     @pl.when(core != bit)
     def _():
-        for copy in across_core:
+        for copy in inner:
             copy.wait_send()
 
-    for copy in sends:
+    @pl.when(core == bit)
+    def _():
+        for _, there in data_hand + map_hand:
+            there.wait_send()
+
+    for copy in sends + copies:
         copy.wait_send()
     mark(None)
 
@@ -626,43 +711,51 @@
     consts = tables(n)
     vmem = pl.BlockSpec(memory_space=pltpu.VMEM)
     smem = pl.BlockSpec(memory_space=pltpu.SMEM)
-    slots = blocks * SPK_DEV
     pair_count = live // 2
     dma = pltpu.SemaphoreType.DMA
-    return pl.pallas_call(
-        functools.partial(kernel, (n, tiles, coils, rows, live)),
-        out_shape=jax.ShapeDtypeStruct((rows, 2, n), F32),
-        in_specs=[smem, smem] + [vmem] * 4 + [pl.BlockSpec(memory_space=pl.ANY)] * len(consts),
-        out_specs=vmem,
-        scratch_shapes=[pltpu.VMEM(c.shape, BF16) for c in consts] + [
-            pltpu.VMEM((SPK_DEV * FIELDS, n), BF16),
-            pltpu.VMEM((blocks, SPK_DEV * FIELDS, n), BF16),
+    any_space = pl.BlockSpec(memory_space=pl.ANY)
+    weights = jnp.transpose(interp_weights, (1, 0, 2))
+    scratch = [pltpu.VMEM(c.shape, BF16) for c in consts] + [
+            pltpu.VMEM(sample_bins.shape, jnp.int32),
+            pltpu.VMEM(kspace_data.shape, BF16),
+            pltpu.VMEM(coil_maps.shape, F32),
+            pltpu.VMEM((FIELDS, SPK_DEV, n), BF16),
+            pltpu.VMEM((blocks, FIELDS, SPK_DEV, n), BF16),
             pltpu.VMEM((SPK_DEV * 2, n), BF16),
             pltpu.VMEM((blocks, SPK_DEV * 2, n), BF16),
             pltpu.VMEM((2, rows, n), F32),
             pltpu.VMEM((2, blocks, rows, n), F32),
-            pltpu.VMEM((n // LANES, slots * FIELDS, LANES), F32),
             pltpu.VMEM((2, 4 * TAPS, pair_count, n), F32),
             pltpu.VMEM((2, 3, pair_count, n), F32),
             pltpu.VMEM((pair_count, 2, n, n), BF16),
             pltpu.VMEM((pair_count, 2, window, n), BF16),
             pltpu.VMEM((2, 2 * window, n), BF16),
             pltpu.VMEM((2, 2 * window, n), F32),
-            pltpu.VMEM((2, 2, 2 * window, GROUP * n), BF16),
+            pltpu.VMEM((2, 2 * window, GROUP * n), BF16),
+            pltpu.VMEM((2, 2 * window, GROUP * n), BF16),
             pltpu.VMEM((2 * n, n), BF16),
             pltpu.VMEM((2 * n, n), BF16),
             pltpu.VMEM((2, n, n), F32),
             pltpu.VMEM((2, 2, coils, 2, n, half), F32),
             pltpu.VMEM((2, 2, n, half), F32),
-            dma((len(consts),)),
-            dma((blocks,)), dma((blocks,)), dma((blocks,)), dma((blocks,)),
-            dma((blocks,)), dma((blocks,)),
+    ]
+    out = pl.pallas_call(
+        functools.partial(kernel, (n, tiles, coils, rows, live)),
+        out_shape=jax.ShapeDtypeStruct((rows * 2 * n // LANES, LANES), F32),
+        in_specs=[smem, smem] + [any_space] * (4 + len(consts)),
+        out_specs=vmem,
+        scratch_shapes=scratch + [
+            dma((len(consts),)), dma((4,)),
+            dma((blocks,)), dma((blocks,)), dma((2 + tiles + blocks,)), dma((blocks,)),
+            dma((2 + tiles + blocks,)), dma((blocks,)),
             dma((2, 2, coils)), dma((2, 2, coils)),
         ],
         compiler_params=pltpu.CompilerParams(
-            has_side_effects=True, collective_id=0, vmem_limit_bytes=60 * 1024 * 1024
+            has_side_effects=True, collective_id=0, vmem_limit_bytes=VMEM_LIMIT
         ),
-    )(thresholds, spoke_count, interp_weights, sample_bins, kspace_data, coil_maps, *consts)
+    )(thresholds, spoke_count, weights, sample_bins, kspace_data, coil_maps, *consts)
+    out = out.reshape(rows, n // LANES, 2, LANES)
+    return jnp.transpose(out, (0, 2, 1, 3)).reshape(rows, 2, n)
 
 
 def solution(mesh):

time: 63.2 us -> 51.6 us (0.82)
  Pallas kernels: 59.4 us -> 48.7 us
  local copies, waits for them, and re-layouts: 2.83 us -> 1.47 us
    pallas_call x1, Pallas kernels: 59.4 us -> 48.7 us  [local(): pl.pallas_call(functools.partial(kernel, (n, tiles, coils, rows, live)),...]
    unnamed x2 -> x1, local copies, waits for them, and re-layouts: 2.83 us -> 1.47 us
where the time goes in v2:
time: 51.6 us; the launch traced here: 50.8 us
  Pallas kernels  48.7 us (94%)
  local copies, waits for them, and re-layouts  1.47 us (3%)
  between operations  0.66 us (1%)
    pallas_call x1, Pallas kernels, local(): pl.pallas_call(functools.partial(kernel, (n, tiles, coils, rows, live)),...  48.7 us
    unnamed x1, local copies, waits for them, and re-layouts  1.47 us

profile of v2, /device:TPU:1, one launch (start us, length us, event | category | flops | bytes accessed | tf_op | source)
XLA Modules:
  0.0 50.8 jit_solution(6474117938961659858)
XLA Ops:
  0.7 48.7 %shard_map.127 = f32[128,128]{1,0:T(8,128)} custom-call(f32[3]{0:T(128)} %thr_ref.1, s32[1]{0:T(128)S(6)} %copy.16.count_ref, bf16[6,8,256]{2,1,0:T(8,128)(2,1)} %bitcast.7, s32[8,256]{1,0:T(8,128)} %bins_hbm.1, bf16[1,8,2,256]{3,2,1,0:T(2,128)(2,1)} %data_hbm.1, f32[1,32,2,256]{3,2,1,0:T(2,128)} %map_hbm.1, bf16[2,256,256]{2,1,0:T(8,128)(2,1)} %constant.14.clone.right_hbm, ...), custom_call_target="tpu_custom_call" | custom-call | tf_op jit(solution)/shard_map/pallas_call | solution.py:742
  49.4 1.5 %copy.17 = f32[32,2,256]{2,1,0:T(2,128)} copy(f32[32,2,256]{2,1,0:T(2,128)} %bitcast.6) | data formatting | bytes 131072

commit v3 on v2

--- a/solution.py
+++ b/solution.py
@@ -14,7 +14,7 @@
 MEMBERS = 2**LEVELS
 ITERS = 4
 CORES = 2
-GROUP = 2
+GROUP = 4
 TAPS = 3
 FIELDS = 8
 MARGIN = 16
@@ -282,11 +282,15 @@
     across = pair * CORES + 1 - bit
     routes = [{"coil": across, "spk": bit}, {"tile": near[1], "spk": bit},
               {"coil": across, "tile": near[1], "spk": bit}]
-    routes += [{"tile": near[d], "spk": bit} for d in far_first if d > 1]
-
-    def spread(src, dst, s_sem, r_sem):
-        for k, route in enumerate(routes):
-            sends.append(send(src, dst, s_sem.at[1 + k], r_sem, route))
+    far = [d for d in far_first if d > 1]
+    even = [d for d in far if d % 2 == 0]
+
+    def outward(distances):
+        return [{"tile": near[d], "spk": bit} for d in distances]
+
+    def spread(src, dst, s_sem, r_sem, targets):
+        for k, target in enumerate(targets):
+            sends.append(send(src, dst, s_sem.at[1 + k], r_sem, target))
         local_copy = pltpu.make_async_copy(src, dst, r_sem)
         inner_copy = pltpu.make_async_remote_copy(
             src_ref=src, dst_ref=dst, send_sem=s_sem.at[0], recv_sem=r_sem,
@@ -302,40 +306,48 @@
         def _():
             inner_copy.start()
 
-    spread(data_mine, data_all.at[block], data_send, data_recv.at[block])
+    spread(data_mine, data_all.at[block], data_send, data_recv.at[block], routes + outward(far))
     const_copies[0].wait()
     for p in range(2):
         map_mine[p] = sum(mm_t(x, perms[0]) for x in split(map_ref[0, :, p, :]))
-    spread(map_mine, maps.at[:, block], map_send, map_recv.at[block])
+    spread(map_mine, maps.at[:, block], map_send, map_recv.at[block], routes[:1] + outward(even) + routes[1:])
 
     def arrived(ref, sem):
         pltpu.make_async_copy(ref, ref, sem).wait()
 
-    def hand_over(ref, s_sem, r_sem):
+    beyond = [{"coil": across}, {"tile": near[1]}, {"coil": across, "tile": near[1]}]
+
+    def hand_over(ref, s_sem, first, r_sem, targets):
         return (
             pltpu.make_async_copy(ref, ref, r_sem),
-            pltpu.make_async_remote_copy(
-                src_ref=ref, dst_ref=ref, send_sem=s_sem, recv_sem=r_sem,
-                device_id={"coil": across}, device_id_type=MESH,
-            ),
+            [
+                pltpu.make_async_remote_copy(
+                    src_ref=ref, dst_ref=ref, send_sem=s_sem.at[first + k], recv_sem=r_sem,
+                    device_id=target, device_id_type=MESH,
+                )
+                for k, target in enumerate(targets)
+            ],
         )
 
     map_hand, data_hand = [], []
-    for d in far_first:
-        if d < 2:
-            continue
+    for d in far:
         for c in range(CORES):
             b = near[d] * CORES + c
-            k = 2 + tiles + len(map_hand)
-            map_hand.append(hand_over(maps.at[:, b], map_send.at[k], map_recv.at[b]))
-            data_hand.append(hand_over(data_all.at[b], data_send.at[k], data_recv.at[b]))
+            data_hand.append(hand_over(
+                data_all.at[b], data_send, 2 + tiles + len(data_hand), data_recv.at[b], beyond[:1]
+            ))
+            if d in even:
+                map_hand.append(hand_over(
+                    maps.at[:, b], map_send, 2 + tiles + 3 * len(map_hand), map_recv.at[b], beyond
+                ))
 
     def pass_on(hands):
         @pl.when(core == bit)
         def _():
             for here, there in hands:
                 here.wait()
-                there.start()
+                for copy in there:
+                    copy.start()
 
     mark("metawait")
     for copy in const_copies[1:]:
@@ -351,16 +363,6 @@
         b = near[d] * CORES + 1 - core
         arrived(meta_all.at[b], meta_recv.at[b])
 
-    mark("pass")
-
-    pass_on(data_hand)
-    direct = [near[d] * CORES + c for d in range(2) for c in range(CORES)]
-
-    @pl.when(core == bit)
-    def _():
-        for b in direct:
-            arrived(data_all.at[b], data_recv.at[b])
-
     mark("rank")
     whole = [meta_all[b].reshape(FIELDS * SPK_DEV, n).astype(F32) for b in range(blocks)]
 
@@ -393,8 +395,6 @@
             for o, value in enumerate(halves(tap.astype(F32))):
                 pairs[o, m + t] = value
 
-    stage = len(map_hand) // 2
-    pass_on(map_hand[:stage])
     mark("build")
 
     def build(i, carry):
@@ -418,10 +418,23 @@
             col_tab[i, o] = table(cells, TAPS, o)
         return carry
 
-    lax.fori_loop(0, pair_count, build, 0)
+    lax.fori_loop(0, pair_count // 2, build, 0)
+
+    mark("pass")
+    pass_on(data_hand)
+    pass_on(map_hand)
+    direct = [near[d] * CORES + c for d in range(2) for c in range(CORES)]
+    last_maps = [near[d] * CORES + c for d in [0] + list(range(1, tiles, 2)) for c in range(CORES)]
+
+    @pl.when(core == bit)
+    def _():
+        for b in direct:
+            arrived(data_all.at[b], data_recv.at[b])
+
+    mark("build2")
+    lax.fori_loop(pair_count // 2, pair_count, build, 0)
 
     mark("datawait")
-    pass_on(map_hand[stage:])
 
     @pl.when(core != bit)
     def _():
@@ -463,6 +476,8 @@
             limit = jnp.where(band == level + 1, thr_ref[level], limit)
         limits.append(limit)
         scales.append(lane_norm * norm_of(k))
+    steps_of = [-STEP_SIZE * scale for scale in scales]
+    own_half = block // (blocks // 2)
 
     copies = []
     for it in range(ITERS):
@@ -543,7 +558,7 @@
 
             @pl.when(core == bit)
             def _():
-                for b in direct:
+                for b in last_maps:
                     arrived(maps.at[:, b], map_recv.at[b])
 
             for p in range(2):
@@ -557,9 +572,13 @@
                     sens[p, q] = both[:, q * half : (q + 1) * half]
 
         mark("image")
+        last = it == ITERS - 1
+        chunks = [own_half] if last else [0, 1]
+        if last:
+            sides = [[jnp.where(own_half == 0, a, b) for a, b in zip(*sides)]]
         copies = []
-        for q in range(2):
-            w = mm3((back[0], back[1]), sides[q])
+        for q, side in zip(chunks, sides):
+            w = mm3((back[0], back[1]), side)
             c_r, c_i, s_r, s_i = w[:half, :half], w[:half, half:], w[half:, :half], w[half:, half:]
             z_r, z_i = jnp.where(first_row, 0.0, s_r), jnp.where(first_row, 0.0, s_i)
             low_r, low_i = c_r - z_i, c_i + z_r
@@ -572,8 +591,17 @@
                 [low_i, pltpu.roll(high_i[:groups], groups - 1, 0), high_i[groups:]], axis=0
             )
             m_r, m_i = sens[0, q], sens[1, q]
-            grads[slot, q, mine, 0] = m_r * d_r + m_i * d_i
-            grads[slot, q, mine, 1] = m_r * d_i - m_i * d_r
+            combined = jnp.concatenate([m_r * d_r + m_i * d_i, m_r * d_i - m_i * d_r], axis=1)
+
+            def piece(x, h, m):
+                first = h * half + (m if h == 0 else (MEMBERS - m) % MEMBERS) * groups
+                return x[first : first + groups]
+
+            along = []
+            for h in range(2):
+                along += forward_haar([piece(combined, h, m) for m in range(MEMBERS)])
+            side = split(jnp.concatenate(along, axis=0))
+            grads[slot, q, mine] = mm(side[0], haar[q, 0]) + mm(side[1], haar[q, 0])
             for d in range(1, coils):
                 d_pair, d_core = d // CORES, d % CORES
                 copy = pltpu.make_async_remote_copy(
@@ -590,8 +618,7 @@
                 copy.start()
                 copies.append(copy)
 
-        coeff_of = []
-        for q in range(2):
+        for q in chunks:
             mark("gradwait")
             for d in range(1, coils):
                 d_pair, d_core = d // CORES, d % CORES
@@ -603,30 +630,20 @@
             summed = grads[slot, q, 0]
             for c in range(1, coils):
                 summed = summed + grads[slot, q, c]
-            target = -STEP_SIZE * jnp.concatenate([summed[0], summed[1]], axis=1)
-            if it > 0:
-                target = estimate[q] + target
-
-            def piece(x, h, m):
-                first = h * half + (m if h == 0 else (MEMBERS - m) % MEMBERS) * groups
-                return x[first : first + groups]
-
-            along = []
-            for h in range(2):
-                along += forward_haar([piece(target, h, m) for m in range(MEMBERS)])
-            side = split(jnp.concatenate(along, axis=0))
-            coeff_of.append(mm(side[0], haar[q, 0]) + mm(side[1], haar[q, 0]))
-        for q in range(2):
-            coeffs = coeff_of[q]
             shrunk = []
             for h in range(2):
                 for k in range(MEMBERS):
-                    first = h * half + k * groups
-                    c_r = coeffs[first : first + groups, :half] * scales[k]
-                    c_i = coeffs[first : first + groups, half:] * scales[k]
+                    at = slice(h * half + k * groups, h * half + (k + 1) * groups)
+                    c_r = summed[at, :half] * steps_of[k]
+                    c_i = summed[at, half:] * steps_of[k]
+                    if it > 0:
+                        c_r, c_i = estimate[q, at, :half] + c_r, estimate[q, at, half:] + c_i
                     power = jnp.maximum(c_r * c_r + c_i * c_i, TINY)
-                    factor = jnp.maximum(1.0 - limits[k] * lax.rsqrt(power), 0.0) * scales[k]
-                    shrunk.append(jnp.concatenate([c_r * factor, c_i * factor], axis=1))
+                    factor = jnp.maximum(1.0 - limits[k] * lax.rsqrt(power), 0.0)
+                    c_r, c_i = c_r * factor, c_i * factor
+                    if not last:
+                        estimate[q, at, :half], estimate[q, at, half:] = c_r, c_i
+                    shrunk.append(jnp.concatenate([c_r * scales[k], c_i * scales[k]], axis=1))
             side = split(jnp.concatenate(shrunk, axis=0))
             along = mm(side[0], haar[q, 1]) + mm(side[1], haar[q, 1])
             fresh = []
@@ -640,7 +657,6 @@
                     placed[m if h == 0 else (MEMBERS - m) % MEMBERS] = members[m]
                 fresh += placed
             fresh = jnp.concatenate(fresh, axis=0)
-            estimate[q] = fresh
             if it < ITERS - 1:
                 mark("fwd")
                 e_r, e_i = fresh[:, :half], fresh[:, half:]
@@ -675,13 +691,12 @@
                 kspace[1, first + half : first + window] = whole[p][:MARGIN]
 
     mark("out")
-    take = lax.broadcasted_iota(jnp.int32, (rows, n), 0) + block * rows
-    at = lax.broadcasted_iota(jnp.int32, (rows, n), 1)
-    owner = jnp.where(at <= half, at, n + half - at)
+    take = lax.broadcasted_iota(jnp.int32, (rows, half), 0) + block * rows
+    at = lax.broadcasted_iota(jnp.int32, (rows, half), 1)
+    owner = jnp.where(own_half == 0, at, jnp.where(at == 0, half, n - at))
     chosen = jnp.where(take == owner, 1.0, 0.0).astype(BF16)
     for p in range(2):
-        mine_rows = jnp.concatenate([estimate[q, :, p * half : (p + 1) * half] for q in range(2)], axis=1)
-        picked = sum(mm_t(chosen, x) for x in split(mine_rows))
+        picked = sum(mm_t(chosen, x) for x in split(fresh[:, p * half : (p + 1) * half]))
         result = sum(mm(x, perms[0]) for x in split(picked))
         for t in range(n // LANES):
             out_ref[pl.ds(t * 2 + p, rows, stride=2 * n // LANES), :] = result[:, t * LANES : (t + 1) * LANES]
@@ -694,7 +709,8 @@
     @pl.when(core == bit)
     def _():
         for _, there in data_hand + map_hand:
-            there.wait_send()
+            for copy in there:
+                copy.wait_send()
 
     for copy in sends + copies:
         copy.wait_send()
@@ -736,7 +752,7 @@
             pltpu.VMEM((2 * n, n), BF16),
             pltpu.VMEM((2 * n, n), BF16),
             pltpu.VMEM((2, n, n), F32),
-            pltpu.VMEM((2, 2, coils, 2, n, half), F32),
+            pltpu.VMEM((2, 2, coils, n, n), F32),
             pltpu.VMEM((2, 2, n, half), F32),
     ]
     out = pl.pallas_call(
@@ -746,8 +762,8 @@
         out_specs=vmem,
         scratch_shapes=scratch + [
             dma((len(consts),)), dma((4,)),
-            dma((blocks,)), dma((blocks,)), dma((2 + tiles + blocks,)), dma((blocks,)),
-            dma((2 + tiles + blocks,)), dma((blocks,)),
+            dma((blocks,)), dma((blocks,)), dma((2 + tiles + 3 * blocks,)), dma((blocks,)),
+            dma((2 + tiles + 3 * blocks,)), dma((blocks,)),
             dma((2, 2, coils)), dma((2, 2, coils)),
         ],
         compiler_params=pltpu.CompilerParams(

time: 51.6 us -> 48 us (0.930); the launches traced: 50.8 us -> 47.8 us
  Pallas kernels: 48.7 us -> 45.6 us
    pallas_call x1, Pallas kernels: 48.7 us -> 45.6 us  [local(): pl.pallas_call(functools.partial(kernel, (n, tiles, coils, rows, live)),...]
where the time goes in v3:
time: 48 us; the launch traced here: 47.8 us
  Pallas kernels  45.6 us (95%)
  local copies, waits for them, and re-layouts  1.47 us (3%)
  between operations  0.66 us (1%)
    pallas_call x1, Pallas kernels, local(): pl.pallas_call(functools.partial(kernel, (n, tiles, coils, rows, live)),...  45.6 us
    unnamed x1, local copies, waits for them, and re-layouts  1.47 us

profile of v3, /device:TPU:1, one launch (start us, length us, event | category | flops | bytes accessed | tf_op | source)
XLA Modules:
  0.0 47.8 jit_solution(6427975558143880680)
XLA Ops:
  0.7 45.6 %shard_map.127 = f32[128,128]{1,0:T(8,128)} custom-call(f32[3]{0:T(128)} %thr_ref.1, s32[1]{0:T(128)S(6)} %copy.16.count_ref, bf16[6,8,256]{2,1,0:T(8,128)(2,1)} %bitcast.7, s32[8,256]{1,0:T(8,128)} %bins_hbm.1, bf16[1,8,2,256]{3,2,1,0:T(2,128)(2,1)} %data_hbm.1, f32[1,32,2,256]{3,2,1,0:T(2,128)} %map_hbm.1, bf16[2,256,256]{2,1,0:T(8,128)(2,1)} %constant.14.clone.right_hbm, ...), custom_call_target="tpu_custom_call" | custom-call | tf_op jit(solution)/shard_map/pallas_call | solution.py:758
  46.3 1.5 %copy.17 = f32[32,2,256]{2,1,0:T(2,128)} copy(f32[32,2,256]{2,1,0:T(2,128)} %bitcast.6) | data formatting | bytes 131072

commit v4 on v3

--- a/solution.py
+++ b/solution.py
@@ -198,6 +198,14 @@
         return value
 
     mark("start")
+    arg_copies = []
+    for k, (src, dst) in enumerate((
+        (bins_hbm, bins_ref), (weight_hbm, meta_mine.at[: 2 * TAPS]),
+        (data_hbm, data_ref), (map_hbm, map_ref),
+    )):
+        copy = pltpu.make_async_copy(src, dst, arg_sem.at[k])
+        copy.start()
+        arg_copies.append(copy)
     barrier = pltpu.get_barrier_semaphore()
     peers = [
         (d_bit, d_tile, d_core)
@@ -227,14 +235,6 @@
             },
             device_id_type=MESH,
         )
-    arg_copies = []
-    for k, (src, dst) in enumerate((
-        (bins_hbm, bins_ref), (weight_hbm, meta_mine.at[: 2 * TAPS]),
-        (data_hbm, data_ref), (map_hbm, map_ref),
-    )):
-        copy = pltpu.make_async_copy(src, dst, arg_sem.at[k])
-        copy.start()
-        arg_copies.append(copy)
     const_copies = []
     for k, (src, dst) in enumerate((
         (perm_hbm, perms), (cell_u_hbm, cell_u), (cell_v_hbm, cell_v), (right_hbm, right),
@@ -245,7 +245,7 @@
         const_copies.append(copy)
 
     mark("prep")
-    for copy in arg_copies:
+    for copy in arg_copies[:2]:
         copy.wait()
     alive = lax.broadcasted_iota(jnp.int32, (SPK_DEV, n), 0) < count_ref[0]
     bins = bins_ref[...]
@@ -253,8 +253,6 @@
     col_of = (bins % n).astype(F32)
     meta_mine[2 * TAPS] = row_of.astype(BF16)
     meta_mine[2 * TAPS + 1] = col_of.astype(BF16)
-    data_wide = data_ref[0].astype(F32)
-    data_mine[...] = jnp.concatenate([data_wide[:, 0], data_wide[:, 1]], axis=0).astype(BF16)
     mark("barrier")
     pl.semaphore_wait(barrier, len(peers) + coils - CORES)
 
@@ -306,8 +304,12 @@
         def _():
             inner_copy.start()
 
+    arg_copies[2].wait()
+    data_wide = data_ref[0].astype(F32)
+    data_mine[...] = jnp.concatenate([data_wide[:, 0], data_wide[:, 1]], axis=0).astype(BF16)
     spread(data_mine, data_all.at[block], data_send, data_recv.at[block], routes + outward(far))
     const_copies[0].wait()
+    arg_copies[3].wait()
     for p in range(2):
         map_mine[p] = sum(mm_t(x, perms[0]) for x in split(map_ref[0, :, p, :]))
     spread(map_mine, maps.at[:, block], map_send, map_recv.at[block], routes[:1] + outward(even) + routes[1:])
@@ -341,8 +343,8 @@
                     maps.at[:, b], map_send, 2 + tiles + 3 * len(map_hand), map_recv.at[b], beyond
                 ))
 
-    def pass_on(hands):
-        @pl.when(core == bit)
+    def pass_on(hands, where):
+        @pl.when((core == bit) & where)
         def _():
             for here, there in hands:
                 here.wait()
@@ -395,6 +397,8 @@
             for o, value in enumerate(halves(tap.astype(F32))):
                 pairs[o, m + t] = value
 
+    mark("pass")
+    pass_on(data_hand + map_hand, tile != 0)
     mark("build")
 
     def build(i, carry):
@@ -421,8 +425,7 @@
     lax.fori_loop(0, pair_count // 2, build, 0)
 
     mark("pass")
-    pass_on(data_hand)
-    pass_on(map_hand)
+    pass_on(data_hand, tile == 0)
     direct = [near[d] * CORES + c for d in range(2) for c in range(CORES)]
     last_maps = [near[d] * CORES + c for d in [0] + list(range(1, tiles, 2)) for c in range(CORES)]
 
@@ -433,6 +436,8 @@
 
     mark("build2")
     lax.fori_loop(pair_count // 2, pair_count, build, 0)
+    mark("pass")
+    pass_on(map_hand, tile == 0)
 
     mark("datawait")
 
@@ -577,8 +582,8 @@
         if last:
             sides = [[jnp.where(own_half == 0, a, b) for a, b in zip(*sides)]]
         copies = []
-        for q, side in zip(chunks, sides):
-            w = mm3((back[0], back[1]), side)
+        products = [mm3((back[0], back[1]), side) for side in sides]
+        for q, w in zip(chunks, products):
             c_r, c_i, s_r, s_i = w[:half, :half], w[:half, half:], w[half:, :half], w[half:, half:]
             z_r, z_i = jnp.where(first_row, 0.0, s_r), jnp.where(first_row, 0.0, s_i)
             low_r, low_i = c_r - z_i, c_i + z_r
@@ -618,6 +623,7 @@
                 copy.start()
                 copies.append(copy)
 
+        shrunken = []
         for q in chunks:
             mark("gradwait")
             for d in range(1, coils):
@@ -644,7 +650,9 @@
                     if not last:
                         estimate[q, at, :half], estimate[q, at, half:] = c_r, c_i
                     shrunk.append(jnp.concatenate([c_r * scales[k], c_i * scales[k]], axis=1))
-            side = split(jnp.concatenate(shrunk, axis=0))
+            shrunken.append(split(jnp.concatenate(shrunk, axis=0)))
+        fresh_of, seen_of = [], []
+        for q, side in zip(chunks, shrunken):
             along = mm(side[0], haar[q, 1]) + mm(side[1], haar[q, 1])
             fresh = []
             for h in range(2):
@@ -657,14 +665,16 @@
                     placed[m if h == 0 else (MEMBERS - m) % MEMBERS] = members[m]
                 fresh += placed
             fresh = jnp.concatenate(fresh, axis=0)
-            if it < ITERS - 1:
-                mark("fwd")
+            fresh_of.append(fresh)
+        if not last:
+            mark("fwd")
+            for q, fresh in zip(chunks, fresh_of):
                 e_r, e_i = fresh[:, :half], fresh[:, half:]
                 m_r, m_i = sens[0, q], sens[1, q]
-                seen = split(
+                seen_of.append(split(
                     jnp.concatenate([m_r * e_r - m_i * e_i, m_r * e_i + m_i * e_r], axis=1)
-                )
-                w = mm3((fore[0], fore[1]), seen)
+                ))
+            for q, w in zip(chunks, [mm3((fore[0], fore[1]), seen) for seen in seen_of]):
                 c_r, c_i, s_r, s_i = w[:half, :half], w[:half, half:], w[half:, :half], w[half:, half:]
                 z_r, z_i = jnp.where(first_row, 0.0, s_r), jnp.where(first_row, 0.0, s_i)
                 v = jnp.concatenate(

time: 48 us -> 46.8 us (0.975)
  Pallas kernels: 45.6 us -> 44.5 us
    pallas_call x1, Pallas kernels: 45.6 us -> 44.5 us  [local(): pl.pallas_call(functools.partial(kernel, (n, tiles, coils, rows, live)),...]
where the time goes in v4:
time: 46.8 us; the launch traced here: 46.6 us
  Pallas kernels  44.5 us (95%)
  local copies, waits for them, and re-layouts  1.47 us (3%)
  between operations  0.66 us (1%)
    pallas_call x1, Pallas kernels, local(): pl.pallas_call(functools.partial(kernel, (n, tiles, coils, rows, live)),...  44.5 us
    unnamed x1, local copies, waits for them, and re-layouts  1.47 us

profile of v4, /device:TPU:1, one launch (start us, length us, event | category | flops | bytes accessed | tf_op | source)
XLA Modules:
  0.0 46.6 jit_solution(9034238529301066396)
XLA Ops:
  0.7 44.5 %shard_map.127 = f32[128,128]{1,0:T(8,128)} custom-call(f32[3]{0:T(128)} %thr_ref.1, s32[1]{0:T(128)S(6)} %copy.16.count_ref, bf16[6,8,256]{2,1,0:T(8,128)(2,1)} %bitcast.7, s32[8,256]{1,0:T(8,128)} %bins_hbm.1, bf16[1,8,2,256]{3,2,1,0:T(2,128)(2,1)} %data_hbm.1, f32[1,32,2,256]{3,2,1,0:T(2,128)} %map_hbm.1, bf16[2,256,256]{2,1,0:T(8,128)(2,1)} %constant.14.clone.right_hbm, ...), custom_call_target="tpu_custom_call" | custom-call | tf_op jit(solution)/shard_map/pallas_call | solution.py:768
  45.2 1.5 %copy.17 = f32[32,2,256]{2,1,0:T(2,128)} copy(f32[32,2,256]{2,1,0:T(2,128)} %bitcast.6) | data formatting | bytes 131072

commit v5 on v4

--- a/solution.py
+++ b/solution.py
@@ -312,7 +312,7 @@
     arg_copies[3].wait()
     for p in range(2):
         map_mine[p] = sum(mm_t(x, perms[0]) for x in split(map_ref[0, :, p, :]))
-    spread(map_mine, maps.at[:, block], map_send, map_recv.at[block], routes[:1] + outward(even) + routes[1:])
+    spread(map_mine, maps.at[:, block], map_send, map_recv.at[block], outward(even) + routes[::-1])
 
     def arrived(ref, sem):
         pltpu.make_async_copy(ref, ref, sem).wait()
@@ -488,7 +488,6 @@
     for it in range(ITERS):
         slot = it % 2
         mark("spokes")
-        grid[...] = jnp.zeros_like(grid)
 
         def fore_step(step, into, it=it):
             for g in range(GROUP):
@@ -507,7 +506,7 @@
                             col * (dens * value)
                         ).astype(BF16)
 
-        def back_step(step, source):
+        def back_step(step, source, opens=False):
             for o in range(2):
                 total = None
                 for g in range(GROUP):
@@ -515,20 +514,23 @@
                         source[o, :, g * n : (g + 1) * n], row_tab[step * GROUP + g, o]
                     )
                     total = added if total is None else total + added
-                grid[o] += total
+                grid[o] = total if opens else grid[o] + total
 
         turns = pair_count // GROUP // 2
         fore_step(0, smear_a)
 
-        def body(turn, carry):
-            back_step(2 * turn, smear_a)
+        def body(turn, carry, opens=False):
+            back_step(2 * turn, smear_a, opens)
             fore_step(2 * turn + 1, smear_b)
             back_step(2 * turn + 1, smear_b)
             fore_step(2 * turn + 2, smear_a)
             return carry
 
-        lax.fori_loop(0, turns - 1, body, 0)
-        back_step(2 * turns - 2, smear_a)
+        if turns > 1:
+            body(0, 0, True)
+            if turns > 2:
+                lax.fori_loop(1, turns - 1, body, 0)
+        back_step(2 * turns - 2, smear_a, turns == 1)
         fore_step(2 * turns - 1, smear_b)
         back_step(2 * turns - 1, smear_b)
 

time: 46.8 us -> 46.8 us (level)
  no operation moved by 1% of the time
where the time goes in v5:
time: 46.8 us; the launch traced here: 46.6 us
  Pallas kernels  44.5 us (95%)
  local copies, waits for them, and re-layouts  1.47 us (3%)
  between operations  0.66 us (1%)
    pallas_call x1, Pallas kernels, local(): pl.pallas_call(functools.partial(kernel, (n, tiles, coils, rows, live)),...  44.5 us
    unnamed x1, local copies, waits for them, and re-layouts  1.47 us

profile of v5, /device:TPU:1, one launch (start us, length us, event | category | flops | bytes accessed | tf_op | source)
XLA Modules:
  0.0 46.6 jit_solution(9750328835606830366)
XLA Ops:
  0.7 44.5 %shard_map.127 = f32[128,128]{1,0:T(8,128)} custom-call(f32[3]{0:T(128)} %thr_ref.1, s32[1]{0:T(128)S(6)} %copy.16.count_ref, bf16[6,8,256]{2,1,0:T(8,128)(2,1)} %bitcast.7, s32[8,256]{1,0:T(8,128)} %bins_hbm.1, bf16[1,8,2,256]{3,2,1,0:T(2,128)(2,1)} %data_hbm.1, f32[1,32,2,256]{3,2,1,0:T(2,128)} %map_hbm.1, bf16[2,256,256]{2,1,0:T(8,128)(2,1)} %constant.14.clone.right_hbm, ...), custom_call_target="tpu_custom_call" | custom-call | tf_op jit(solution)/shard_map/pallas_call | solution.py:770
  45.2 1.5 %copy.17 = f32[32,2,256]{2,1,0:T(2,128)} copy(f32[32,2,256]{2,1,0:T(2,128)} %bitcast.6) | data formatting | bytes 131072
